TPU v7x, 8 devices: a whole 2x2x1 slice. The times are simulated.
8 devices in a mesh: rep: 1 (over z), y: 2 (over y), x: 4 (over x, core).
Axes of the slice: x: 2, y: 2, z: 1, core: 2. Of those that a mesh axis runs over, the one named last changes fastest.
Arguments:
- hidden: bfloat16 [64, 4096], P('rep', 'y')
- lengths: int32 [64], P('rep')
- k_cache: bfloat16 [2, 64, 128, 32, 128], P(None, ('rep', 'y'), None, 'x')
- v_cache: bfloat16 [2, 64, 128, 32, 128], P(None, ('rep', 'y'), None, 'x')
- rel_table: bfloat16 [2, 128, 32, 128], P(None, None, 'x')
- norm_attn: bfloat16 [2, 4096], P(None, 'y')
- w_q: bfloat16 [2, 4096, 32, 128], P(None, 'y', 'x')
- w_k: bfloat16 [2, 4096, 32, 128], P(None, 'y', 'x')
- w_v: bfloat16 [2, 4096, 32, 128], P(None, 'y', 'x')
- bias_content: bfloat16 [2, 32, 128], P(None, 'x')
- bias_pos: bfloat16 [2, 32, 128], P(None, 'x')
- w_out: bfloat16 [2, 32, 128, 4096], P(None, 'x', None, 'y')
- norm_mlp: bfloat16 [2, 4096], P(None, 'y')
- w_up: bfloat16 [2, 4096, 16384], P(None, 'y', 'x')
- w_down: bfloat16 [2, 16384, 4096], P(None, 'x', 'y')
Outputs:
- output 1: bfloat16 [64, 4096], P('rep', 'y')
- output 2: bfloat16 [2, 64, 128, 32, 128], P(None, ('rep', 'y'), None, 'x')
- output 3: bfloat16 [2, 64, 128, 32, 128], P(None, ('rep', 'y'), None, 'x')
All inputs are finite; a program needn't handle non-finite values.
Results may differ from a plain program's by a relative error of at most 0.0187194.
Values are sent between devices in bfloat16 or wider.
A program may use at most 1 GiB of HBM per device.

v0:
```python
import jax
import jax.numpy as jnp
from jax import lax
from jax.sharding import PartitionSpec as P

EPS = 1e-6


def sharded_norm(hidden, gain, d_total):
    hidden_wide = hidden.astype(jnp.float32)
    sum_sq = lax.psum(jnp.sum(hidden_wide * hidden_wide, axis=1, keepdims=True), "y")
    inv_rms = lax.rsqrt(sum_sq / d_total + EPS)
    return (hidden_wide * inv_rms * gain.astype(jnp.float32)).astype(jnp.bfloat16)


def shift_rel(rel_all, lengths):
    seq_len = rel_all.shape[2]
    padded = jnp.pad(rel_all[:, :, ::-1], ((0, 0), (0, 0), (0, seq_len)))
    return jax.vmap(lambda rel_row, start_at: lax.dynamic_slice_in_dim(rel_row, start_at, seq_len, axis=1))(padded, seq_len - 1 - lengths)


def write_rows(cache_layer, new_rows, lengths):
    hit_mask = jnp.arange(cache_layer.shape[1])[None, :] == lengths[:, None]
    return jnp.where(hit_mask[:, :, None, None], new_rows[:, None, :, :], cache_layer)


def attend(q_rows, k_rows, v_rows, lengths, rel_layer, content_bias, pos_bias):
    q_wide = q_rows.astype(jnp.float32)
    q_content = (q_wide + content_bias.astype(jnp.float32)).astype(jnp.bfloat16)
    q_pos = (q_wide + pos_bias.astype(jnp.float32)).astype(jnp.bfloat16)
    scores = jnp.einsum("bhe,bshe->bhs", q_content, k_rows, preferred_element_type=jnp.float32)
    rel_all = jnp.einsum("bhe,the->bht", q_pos, rel_layer, preferred_element_type=jnp.float32)
    scores = (scores + shift_rel(rel_all, lengths)) * (q_rows.shape[2] ** -0.5)
    in_range = jnp.arange(k_rows.shape[1])[None, None, :] <= lengths[:, None, None]
    attn_prob = jax.nn.softmax(jnp.where(in_range, scores, -1e30), axis=-1).astype(jnp.bfloat16)
    return jnp.einsum("bhs,bshe->bhe", attn_prob, v_rows, preferred_element_type=jnp.float32).astype(jnp.bfloat16)


def solution(mesh):
    y_size = mesh.shape["y"]
    cache_spec = P(None, ("rep", "y"), None, "x", None)
    row_spec = P("rep", "y")
    proj_spec = P(None, "y", "x", None)
    head_spec = P(None, "x", None)
    in_specs = (row_spec, P("rep"), cache_spec, cache_spec, P(None, None, "x", None), P(None, "y"),
                proj_spec, proj_spec, proj_spec, head_spec, head_spec, P(None, "x", None, "y"),
                P(None, "y"), P(None, "y", "x"), P(None, "x", "y"))
    out_specs = (row_spec, cache_spec, cache_spec)

    def local_step(hidden, lengths, k_cache, v_cache, rel_table, norm_attn, w_q, w_k, w_v, bias_content, bias_pos, w_out, norm_mlp, w_up, w_down):
        rows_local = k_cache.shape[1]
        row_start = lax.axis_index("y") * rows_local
        len_local = lax.dynamic_slice_in_dim(lengths, row_start, rows_local)
        d_total = hidden.shape[1] * y_size
        k_layers = []
        v_layers = []
        for layer in range(k_cache.shape[0]):
            normed = sharded_norm(hidden, norm_attn[layer], d_total)
            q_part = jnp.einsum("bd,dhe->bhe", normed, w_q[layer], preferred_element_type=jnp.float32).astype(jnp.bfloat16)
            k_part = jnp.einsum("bd,dhe->bhe", normed, w_k[layer], preferred_element_type=jnp.float32).astype(jnp.bfloat16)
            v_part = jnp.einsum("bd,dhe->bhe", normed, w_v[layer], preferred_element_type=jnp.float32).astype(jnp.bfloat16)
            q_full, k_full, v_full = lax.psum((q_part, k_part, v_part), "y")
            q_rows = lax.dynamic_slice_in_dim(q_full, row_start, rows_local)
            k_rows = lax.dynamic_slice_in_dim(k_full, row_start, rows_local)
            v_rows = lax.dynamic_slice_in_dim(v_full, row_start, rows_local)
            k_new = write_rows(k_cache[layer], k_rows, len_local)
            v_new = write_rows(v_cache[layer], v_rows, len_local)
            k_layers.append(k_new)
            v_layers.append(v_new)
            context = attend(q_rows, k_new, v_new, len_local, rel_table[layer], bias_content[layer], bias_pos[layer])
            context_all = lax.all_gather(context, "y", axis=0, tiled=True)
            attn_part = jnp.einsum("bhe,hed->bd", context_all, w_out[layer], preferred_element_type=jnp.float32).astype(jnp.bfloat16)
            attn_out = lax.psum(attn_part, "x")
            hidden = (hidden.astype(jnp.float32) + attn_out.astype(jnp.float32)).astype(jnp.bfloat16)
            normed = sharded_norm(hidden, norm_mlp[layer], d_total)
            up_part = jnp.dot(normed, w_up[layer], preferred_element_type=jnp.float32).astype(jnp.bfloat16)
            up_proj = lax.psum(up_part, "y")
            activated = jax.nn.gelu(up_proj.astype(jnp.float32), approximate=True).astype(jnp.bfloat16)
            down_part = jnp.dot(activated, w_down[layer], preferred_element_type=jnp.float32).astype(jnp.bfloat16)
            down_out = lax.psum(down_part, "x")
            hidden = (hidden.astype(jnp.float32) + down_out.astype(jnp.float32)).astype(jnp.bfloat16)
        return hidden, jnp.stack(k_layers), jnp.stack(v_layers)

    return jax.shard_map(local_step, mesh=mesh, in_specs=in_specs, out_specs=out_specs, check_vma=False)
```

profile of v0, /device:TPU:0, one launch (start us, length us, event | category | flops | bytes accessed | tf_op | source)
XLA Modules:
  0.0 394.4 jit_solution(17425257984160332906)
XLA Ops:
  7.2 1.1 fusion.82
  8.3 6.3 %psum.112 = f32[64,1]{0,1:T(1,128)S(1)} all-reduce(f32[64,1]{0,1:T(1,128)S(1)} %bitcast.179), channel_id=1, replica_groups=mesh['rep'=1,'y'=2,'x'=4] {'y'}, use_global_device_ids=true, to_apply=%region_1.0 | all-reduce | flops 64 | bytes 512 | tf_op jit(solution)/shard_map/psum | solution.py:11
  14.6 0.9 slice_convert_fusion.1
  15.5 5.5 %fusion.153 = (bf16[1,2048,8,128]{3,2,1,0:T(8,128)(2,1)S(1)}, bf16[1,2048,8,128]{3,2,1,0:T(8,128)(2,1)}) fusion(bf16[2,2048,8,128]{3,2,1,0:T(8,128)(2,1)} %param.21), kind=kLoop, calls=%fused_computation.196 | loop fusion | bytes 16777216 | tf_op jit(solution)/shard_map/slice | solution.py:59
  21.0 1.3 slice-done.1
  22.3 2.4 fusion.152
  24.7 1.5 fusion.60
  26.3 1.5 fusion.61
  27.8 2.2 fusion.151
  30.0 1.5 fusion.62
  32.3 20.9 %all-reduce.28.cloned.1.call-done = (bf16[64,8,128]{2,0,1:T(8,128)(2,1)}, bf16[64,8,128]{2,0,1:T(8,128)(2,1)}, bf16[64,8,128]{2,0,1:T(8,128)(2,1)}) async-done(((bf16[64,8,128]{2,0,1:T(8,128)(2,1)}, bf16[64,8,128]{2,0,1:T(8,128)(2,1)}, bf16[64,8,128]{2,0,1:T(8,128)(2,1)}), (bf16[64,8,128]{2,0,1:T(8,128)(2,1)}, bf16[64,8,128]{2,0,1:T(8,128)(2,1)}, ...) | async-done | bytes 393232 | tf_op jit(solution)/shard_map/psum | solution.py:62
  53.3 1.1 convolution_bitcast_fusion.1
  54.4 0.9 constant_dynamic-slice_fusion.1
  55.4 0.9 fusion.121
  56.4 1.9 copy.87
  58.2 2.5 pad.8.clone
  60.7 4.9 %gather_fusion = f32[32,8,128]{1,0,2:T(8,128)S(1)} fusion(f32[32,8,256]{1,0,2:T(8,128)} %pad.8.clone, s32[32]{0:T(128)S(1)} %get-tuple-element.15), kind=kCustom, calls=%fused_computation | custom fusion | bytes 262528 | tf_op jit(solution)/shard_map/vmap()/gather | solution.py:19
  65.6 11.6 %multiply_reduce_fusion.1 = f32[32,8,128]{1,2,0:T(8,128)S(1)} fusion(f32[32,8,128]{2,1,0:T(8,128)S(1)} %copy.85, pred[32,128]{1,0:T(8,128)(4,1)S(1)} %get-tuple-element.40, bf16[2,32,128,8,128]{4,3,2,1,0:T(8,128)(2,1)} %param.17, bf16[32,8,128]{2,1,0:T(8,128)(2,1)S(1)} %copy.41), kind=kLoop, calls=%fused_computation.13 | loop fusion | flops 16744448 | bytes 8720384
  77.2 2.7 fusion.149
  80.0 0.4 fusion.58
  80.7 1.3 copy.64
  82.0 6.8 %bitcast_select_fusion.2 = bf16[32,128,8,128]{3,2,1,0:T(8,128)(2,1)S(1)} fusion(pred[32,128]{1,0:T(8,128)(4,1)S(1)} %get-tuple-element.40, bf16[2,32,128,8,128]{4,3,2,1,0:T(8,128)(2,1)} %param.18, bf16[32,8,128]{2,1,0:T(8,128)(2,1)S(1)} %copy.45), kind=kLoop, calls=%fused_computation.21 | loop fusion | flops 4194304 | bytes 16846848 | tf_op jit(solution)/shard_map/jit(_where)/select_n | solution.py:24
  88.8 2.3 fusion.16
  91.1 4.9 %all_gather.6 = bf16[64,8,128]{2,0,1:T(8,128)(2,1)S(1)} all-gather(bf16[32,8,128]{2,0,1:T(8,128)(2,1)S(1)} %bitcast.168), channel_id=1, replica_groups=mesh['rep'=1,'y'=2,'x'=4] {'y'}, dimensions={0}, use_global_device_ids=true | all-gather | bytes 196608 | tf_op jit(solution)/shard_map/all_gather | solution.py:71
  96.1 3.7 fusion.45
  99.9 26.7 %all-reduce.14.cloned.1.call-done = bf16[64,2048]{1,0:T(8,128)(2,1)} async-done(((bf16[64,2048]{1,0:T(8,128)(2,1)}), bf16[64,2048]{1,0:T(8,128)(2,1)}) %all-reduce.14.cloned.1.call-update) | async-done | bytes 262160 | tf_op jit(solution)/shard_map/psum | solution.py:73
  126.6 1.1 fusion.86
  127.7 5.5 %psum.117 = f32[64,1]{0,1:T(1,128)S(1)} all-reduce(f32[64,1]{0,1:T(1,128)S(1)} %bitcast.180), channel_id=1, replica_groups=mesh['rep'=1,'y'=2,'x'=4] {'y'}, use_global_device_ids=true, to_apply=%region_9.10 | all-reduce | flops 64 | bytes 512 | tf_op jit(solution)/shard_map/psum | solution.py:11
  133.2 9.8 %fusion.18 = bf16[64,4096]{1,0:T(8,128)(2,1)} fusion(bf16[2,2048,4096]{2,1,0:T(8,128)(2,1)} %param.28, f32[2048]{0:T(1024)S(1)} %bitcast.177, f32[64]{0:T(128)S(1)} %rsqrt_bitcast_fusion.2, bf16[64,2048]{1,0:T(8,128)(2,1)S(1)} %copy-done.2, bf16[64,2048]{1,0:T(8,128)(2,1)} %all-reduce.14.cloned.1.call-done), kind=kOutput, calls=%fused_computation.32 | convolution fusion | flops 1075052544 | bytes 17834240 | tf_op jit(solution)/shard_map/dot_general | solution.py:76
  143.1 22.9 %all-reduce.16.cloned.1.call-done = bf16[64,4096]{1,0:T(8,128)(2,1)} async-done(((bf16[64,4096]{1,0:T(8,128)(2,1)}), bf16[64,4096]{1,0:T(8,128)(2,1)}) %all-reduce.16.cloned.1.call-update) | async-done | bytes 524304 | tf_op jit(solution)/shard_map/psum | solution.py:77
  166.0 9.7 %fusion.48 = bf16[64,2048]{1,0:T(8,128)(2,1)} fusion(bf16[2,4096,2048]{2,1,0:T(8,128)(2,1)} %param.29, bf16[64,4096]{1,0:T(8,128)(2,1)} %all-reduce.16.cloned.1.call-done), kind=kOutput, calls=%fused_computation.56 | convolution fusion | flops 1076494336 | bytes 17563648 | tf_op jit(solution)/shard_map/dot_general | solution.py:79
  175.8 26.7 %all-reduce.18.cloned.1.call-done = bf16[64,2048]{1,0:T(8,128)(2,1)} async-done(((bf16[64,2048]{1,0:T(8,128)(2,1)}), bf16[64,2048]{1,0:T(8,128)(2,1)}) %all-reduce.18.cloned.1.call-update) | async-done | bytes 262160 | tf_op jit(solution)/shard_map/psum | solution.py:80
  202.5 1.2 fusion.90
  203.7 4.9 %psum.120 = f32[64,1]{0,1:T(1,128)S(1)} all-reduce(f32[64,1]{0,1:T(1,128)S(1)} %bitcast.178), channel_id=1, replica_groups=mesh['rep'=1,'y'=2,'x'=4] {'y'}, use_global_device_ids=true, to_apply=%region_13.14 | all-reduce | flops 64 | bytes 512 | tf_op jit(solution)/shard_map/psum | solution.py:11
  208.6 3.9 fusion.64
  212.5 1.5 fusion.65
  214.0 1.5 fusion.63
  215.8 20.0 %all-reduce.26.cloned.1.call-done = (bf16[64,8,128]{2,0,1:T(8,128)(2,1)}, bf16[64,8,128]{2,0,1:T(8,128)(2,1)}, bf16[64,8,128]{2,0,1:T(8,128)(2,1)}) async-done(((bf16[64,8,128]{2,0,1:T(8,128)(2,1)}, bf16[64,8,128]{2,0,1:T(8,128)(2,1)}, bf16[64,8,128]{2,0,1:T(8,128)(2,1)}), (bf16[64,8,128]{2,0,1:T(8,128)(2,1)}, bf16[64,8,128]{2,0,1:T(8,128)(2,1)}, ...) | async-done | bytes 393232 | tf_op jit(solution)/shard_map/psum | solution.py:62
  235.8 1.1 convolution_bitcast_fusion
  237.0 0.9 constant_dynamic-slice_fusion
  237.9 0.9 constant_dynamic-slice_fusion.2
  238.7 0.9 fusion.119
  239.7 1.9 copy.88
  241.6 2.5 pad.9.clone
  244.1 4.9 %gather_fusion.1 = f32[32,8,128]{1,0,2:T(8,128)S(1)} fusion(f32[32,8,256]{1,0,2:T(8,128)} %pad.9.clone, s32[32]{0:T(128)S(1)} %get-tuple-element.15), kind=kCustom, calls=%fused_computation.1 | custom fusion | bytes 262528 | tf_op jit(solution)/shard_map/vmap()/gather | solution.py:19
  249.0 11.6 %multiply_reduce_fusion = f32[32,8,128]{1,2,0:T(8,128)S(1)} fusion(f32[32,8,128]{2,1,0:T(8,128)S(1)} %copy.86, pred[32,128]{1,0:T(8,128)(4,1)S(1)} %get-tuple-element.40, bf16[2,32,128,8,128]{4,3,2,1,0:T(8,128)(2,1)} %param.17, bf16[32,8,128]{2,1,0:T(8,128)(2,1)S(1)} %copy.48), kind=kLoop, calls=%fused_computation.12 | loop fusion | flops 16744448 | bytes 8720384
  260.6 2.7 fusion.146
  263.4 0.4 fusion.59
  264.1 1.3 copy.74
  265.4 6.8 %bitcast_select_fusion = bf16[32,128,8,128]{3,2,1,0:T(8,128)(2,1)S(1)} fusion(pred[32,128]{1,0:T(8,128)(4,1)S(1)} %get-tuple-element.40, bf16[2,32,128,8,128]{4,3,2,1,0:T(8,128)(2,1)} %param.18, bf16[32,8,128]{2,1,0:T(8,128)(2,1)S(1)} %copy.52), kind=kLoop, calls=%fused_computation.18 | loop fusion | flops 4194304 | bytes 16846848 | tf_op jit(solution)/shard_map/jit(_where)/select_n | solution.py:24
  272.2 2.3 fusion.14
  274.5 4.9 %all_gather.7 = bf16[64,8,128]{2,0,1:T(8,128)(2,1)S(1)} all-gather(bf16[32,8,128]{2,0,1:T(8,128)(2,1)S(1)} %bitcast.169), channel_id=1, replica_groups=mesh['rep'=1,'y'=2,'x'=4] {'y'}, dimensions={0}, use_global_device_ids=true | all-gather | bytes 196608 | tf_op jit(solution)/shard_map/all_gather | solution.py:71
  279.5 3.7 fusion.42
  283.3 22.8 %broadcast_select_fusion.1 = (bf16[1,32,128,8,128]{4,3,2,1,0:T(8,128)(2,1)}, bf16[1,32,128,8,128]{4,3,2,1,0:T(8,128)(2,1)}, bf16[1,32,128,8,128]{4,3,2,1,0:T(8,128)(2,1)}, bf16[1,32,128,8,128]{4,3,2,1,0:T(8,128)(2,1)}) fusion(pred[32,128]{1,0:T(8,128)(4,1)S(1)} %get-tuple-element.40, bf16[2,32,128,8,128]{4,3,2,1,0:T(8,128)(2,1)} %param.18, ...), kind=kLoop, calls=%fused_computation.29 | loop fusion | flops 16777216 | bytes 67375104 | tf_op jit(solution)/shard_map/jit(_where)/select_n | solution.py:24
  306.1 3.9 all-reduce.20.cloned.1.call-done
  310.0 1.1 fusion.94
  311.1 5.1 %psum.125 = f32[64,1]{0,1:T(1,128)S(1)} all-reduce(f32[64,1]{0,1:T(1,128)S(1)} %bitcast.181), channel_id=1, replica_groups=mesh['rep'=1,'y'=2,'x'=4] {'y'}, use_global_device_ids=true, to_apply=%region_21.22 | all-reduce | flops 64 | bytes 512 | tf_op jit(solution)/shard_map/psum | solution.py:11
  316.3 9.9 %fusion.21 = bf16[64,4096]{1,0:T(8,128)(2,1)} fusion(bf16[2,2048,4096]{2,1,0:T(8,128)(2,1)} %param.28, f32[2048]{0:T(1024)S(1)} %bitcast.173, f32[64]{0:T(128)S(1)} %rsqrt_bitcast_fusion, bf16[64,2048]{1,0:T(8,128)(2,1)S(1)} %get-tuple-element.12, bf16[64,2048]{1,0:T(8,128)(2,1)} %all-reduce.20.cloned.1.call-done), kind=kOutput, calls=%fused_computation.33 | convolution fusion | flops 1075052544 | bytes 17834240 | tf_op jit(solution)/shard_map/dot_general | solution.py:76
  326.2 13.8 %pad_maximum_fusion.1 = bf16[2,32,128,8,128]{4,3,2,1,0:T(8,128)(2,1)} fusion(bf16[1,32,128,8,128]{4,3,2,1,0:T(8,128)(2,1)} %get-tuple-element.18, bf16[1,32,128,8,128]{4,3,2,1,0:T(8,128)(2,1)} %get-tuple-element.17), kind=kLoop, calls=%fused_computation.3 | loop fusion | flops 8388608 | bytes 33554432 | tf_op jit(solution)/shard_map/stack | solution.py:82
  340.0 9.1 %all-reduce.22.cloned.1.call-done = bf16[64,4096]{1,0:T(8,128)(2,1)} async-done(((bf16[64,4096]{1,0:T(8,128)(2,1)}), bf16[64,4096]{1,0:T(8,128)(2,1)}) %all-reduce.22.cloned.1.call-update) | async-done | bytes 524304 | tf_op jit(solution)/shard_map/psum | solution.py:77
  349.2 9.7 %fusion.51 = bf16[64,2048]{1,0:T(8,128)(2,1)} fusion(bf16[2,4096,2048]{2,1,0:T(8,128)(2,1)} %param.29, bf16[64,4096]{1,0:T(8,128)(2,1)} %all-reduce.22.cloned.1.call-done), kind=kOutput, calls=%fused_computation.57 | convolution fusion | flops 1076494336 | bytes 17563648 | tf_op jit(solution)/shard_map/dot_general | solution.py:79
  358.9 13.8 %pad_maximum_fusion = bf16[2,32,128,8,128]{4,3,2,1,0:T(8,128)(2,1)} fusion(bf16[1,32,128,8,128]{4,3,2,1,0:T(8,128)(2,1)} %get-tuple-element.33, bf16[1,32,128,8,128]{4,3,2,1,0:T(8,128)(2,1)} %get-tuple-element.34), kind=kLoop, calls=%fused_computation.2 | loop fusion | flops 8388608 | bytes 33554432 | tf_op jit(solution)/shard_map/stack | solution.py:82
  372.7 12.9 %all-reduce.24.cloned.1.call-done = bf16[64,2048]{1,0:T(8,128)(2,1)} async-done(((bf16[64,2048]{1,0:T(8,128)(2,1)}), bf16[64,2048]{1,0:T(8,128)(2,1)}) %all-reduce.24.cloned.1.call-update) | async-done | bytes 262160 | tf_op jit(solution)/shard_map/psum | solution.py:80
  385.6 1.7 fusion.97
  (68 shorter events, 2.6 us)
Async XLA Ops:
  7.2 46.1 %all-reduce.28.cloned.1.call-start = ((), (), s32[]{:S(2)}) async-start(), calls=%async_computation.7 | async-start | bytes 786432 | tf_op jit(solution)/shard_map/psum | solution.py:62
  14.6 6.4 %slice-start = ((s8[8388608]{0:T(1024)(128)(4,1)}), s8[4194304]{0:T(1024)(128)(4,1)S(1)}, s32[]{:S(2)}) async-start(s8[8388608]{0:T(1024)(128)(4,1)} %bitcast.164), calls=%async_computation.8 | async-start | bytes 8388608
  15.5 6.8 %slice-start.1 = ((s8[8388608]{0:T(1024)(128)(4,1)}), s8[4194304]{0:T(1024)(128)(4,1)S(1)}, s32[]{:S(2)}) async-start(s8[8388608]{0:T(1024)(128)(4,1)} %bitcast.164), calls=%async_computation.9 | async-start | bytes 8388608
  15.5 12.3 %slice-start.2 = ((s8[8388608]{0:T(1024)(128)(4,1)}), s8[4194304]{0:T(1024)(128)(4,1)S(1)}, s32[]{:S(2)}) async-start(s8[8388608]{0:T(1024)(128)(4,1)} %bitcast.166), calls=%async_computation.10 | async-start | bytes 8388608
  22.3 2.4 copy-start.2
  22.3 5.5 %slice-start.3 = ((s8[8388608]{0:T(1024)(128)(4,1)}), s8[4194304]{0:T(1024)(128)(4,1)S(1)}, s32[]{:S(2)}) async-start(s8[8388608]{0:T(1024)(128)(4,1)} %bitcast.166), calls=%async_computation.11 | async-start | bytes 8388608
  30.0 1.9 copy-start.9
  30.0 2.1 copy-start.7
  30.0 2.2 copy-start.8
  30.0 2.3 copy-start.5
  31.6 95.0 %all-reduce.14.cloned.1.call-start = ((), (), s32[]{:S(2)}) async-start(), calls=%async_computation | async-start | bytes 524288 | tf_op jit(solution)/shard_map/psum | solution.py:73
  91.1 8.8 %copy-start.6 = (bf16[2,2048]{1,0:T(2,128)(2,1)S(1)}, bf16[2,2048]{1,0:T(2,128)(2,1)}, u32[]{:S(2)}) copy-start(bf16[2,2048]{1,0:T(2,128)(2,1)} %param.27) | copy-start | bytes 24580
  99.8 66.2 %all-reduce.16.cloned.1.call-start = ((), (), s32[]{:S(2)}) async-start(), calls=%async_computation.1 | async-start | bytes 1048576 | tf_op jit(solution)/shard_map/psum | solution.py:77
  143.0 59.5 %copy-start.4 = (bf16[64,2048]{1,0:T(8,128)(2,1)S(1)}, bf16[64,2048]{1,0:T(8,128)(2,1)}, u32[]{:S(2)}) copy-start(bf16[64,2048]{1,0:T(8,128)(2,1)} %all-reduce.14.cloned.1.call-done) | copy-start | bytes 786436
  143.0 59.4 %all-reduce.18.cloned.1.call-start = ((), (), s32[]{:S(2)}) async-start(), calls=%async_computation.2 | async-start | bytes 524288 | tf_op jit(solution)/shard_map/psum | solution.py:80
  175.7 60.1 %all-reduce.26.cloned.1.call-start = ((), (), s32[]{:S(2)}) async-start(), calls=%async_computation.6 | async-start | bytes 786432 | tf_op jit(solution)/shard_map/psum | solution.py:62
  208.6 3.9 copy-start.1
  208.6 5.4 %copy-start = (bf16[1,2048,8,128]{3,2,1,0:T(8,128)(2,1)S(1)}, bf16[1,2048,8,128]{3,2,1,0:T(8,128)(2,1)}, u32[]{:S(2)}) copy-start(bf16[1,2048,8,128]{3,2,1,0:T(8,128)(2,1)} %get-tuple-element.26) | copy-start | bytes 12582916
  215.6 94.4 %all-reduce.20.cloned.1.call-start = ((), (), s32[]{:S(2)}) async-start(), calls=%async_computation.3 | async-start | bytes 524288 | tf_op jit(solution)/shard_map/psum | solution.py:73
  283.2 65.9 %all-reduce.22.cloned.1.call-start = ((), (), s32[]{:S(2)}) async-start(), calls=%async_computation.4 | async-start | bytes 1048576 | tf_op jit(solution)/shard_map/psum | solution.py:77
  326.2 59.5 %all-reduce.24.cloned.1.call-start = ((), (), s32[]{:S(2)}) async-start(), calls=%async_computation.5 | async-start | bytes 524288 | tf_op jit(solution)/shard_map/psum | solution.py:80
  358.9 26.7 %copy-start.3 = (bf16[64,2048]{1,0:T(8,128)(2,1)S(1)}, bf16[64,2048]{1,0:T(8,128)(2,1)}, u32[]{:S(2)}) copy-start(bf16[64,2048]{1,0:T(8,128)(2,1)} %all-reduce.20.cloned.1.call-done) | copy-start | bytes 786436
Sparse Core Ops, SparseCore 0:
  31.7 21.5 all-reduce.27
  100.0 26.5 all-reduce.13
  143.1 22.8 all-reduce.15
  175.9 26.5 all-reduce.17
  215.7 20.0 all-reduce.25
  283.4 26.5 all-reduce.19
  326.3 22.8 all-reduce.21
  359.0 26.5 all-reduce.23
where the time goes:
time: 398 us; the launch traced here: 394 us
  waiting for transfers between devices  143 us (36%)
  other arithmetic  103 us (26%)
  matrix products  64.8 us (16%)
  local copies, waits for them, and re-layouts  35.8 us (9%)
  blocking collectives  31.7 us (8%)
  between operations  14.7 us (4%)
    psum x2, waiting for transfers between devices, local_step(): q_full, k_full, v_full = lax.psum((q_part, k_part, v_part), 'y')  40.9 us
    psum x2, waiting for transfers between devices, local_step(): down_out = lax.psum(down_part, 'x')  39.6 us
    select_n x3, other arithmetic, write_rows(): jnp.where(hit_mask[:, :, None, None], new_rows[:, None, :, :], cache_layer)  36.4 us
    psum x2, waiting for transfers between devices, local_step(): up_proj = lax.psum(up_part, 'y')  32.1 us
    psum x2, waiting for transfers between devices, local_step(): attn_out = lax.psum(attn_part, 'x')  30.5 us
    another operation x2, other arithmetic, local_step(): return (hidden, jnp.stack(k_layers), jnp.stack(v_layers))  27.7 us
    unnamed x6, other arithmetic  24.9 us
    psum x4, blocking collectives, sharded_norm(): lax.psum(jnp.sum(hidden_wide * hidden_wide, axis=1, keepdims=True), 'y')  21.8 us
  transfers between devices with their start and end apart: 8, of which 8 were waited for; matrix products, arithmetic and copies ran while one was open for 13% of the time, Pallas kernels for 0%

commit v1 on v0

v1 whole, which is shorter than its diff:
```python
import functools
import jax
import jax.numpy as jnp
from jax import lax
from jax.experimental import pallas as pl
from jax.experimental.pallas import tpu as pltpu
from jax.sharding import PartitionSpec as P

BF = jnp.bfloat16
F32 = jnp.float32

EPS = 1e-6


def sharded_norm(hidden, gain, d_total):
    hidden_wide = hidden.astype(jnp.float32)
    sum_sq = lax.psum(jnp.sum(hidden_wide * hidden_wide, axis=1, keepdims=True), "y")
    inv_rms = lax.rsqrt(sum_sq / d_total + EPS)
    return (hidden_wide * inv_rms * gain.astype(jnp.float32)).astype(jnp.bfloat16)


def attn_body(layer, group, len_ref, q_ref, kn_ref, vn_ref, rel_ref, u_ref, w_ref, kc, vc, *rest):
    ctx_ref, ko, vo, kbuf, vbuf, rext, rsem, wsem = rest[-8:]
    rows, seq, heads, hd = kbuf.shape
    y = lax.axis_index("y")
    n_grp = rows // group
    span = seq * heads

    def load(i):
        sl = pl.ds(i * group, group)
        return (pltpu.make_async_copy(kc.at[layer, sl], kbuf.at[sl], rsem.at[0, i]),
                pltpu.make_async_copy(vc.at[layer, sl], vbuf.at[sl], rsem.at[1, i]))

    def save(i):
        sl = pl.ds(i * group, group)
        return (pltpu.make_async_copy(kbuf.at[sl], ko.at[layer, sl], wsem.at[0, i]),
                pltpu.make_async_copy(vbuf.at[sl], vo.at[layer, sl], wsem.at[1, i]))

    @pl.loop(0, n_grp)
    def _(i):
        for c in load(i):
            c.start()

    @pl.loop(0, seq)
    def _(t):
        rext[seq - 1 - t] = rel_ref[layer, t]
        rext[seq + t] = jnp.zeros((heads, hd), BF)

    col = lax.broadcasted_iota(jnp.int32, (heads, span), 1)
    row = lax.broadcasted_iota(jnp.int32, (heads, span), 0)
    own = (col % heads) == row
    pos = col // heads
    scale = hd ** -0.5

    @pl.loop(0, n_grp)
    def _(i):
        for c in load(i):
            c.wait()
        outs = []
        for g in range(group):
            b = i * group + g
            ln = len_ref[y * rows + b]
            kbuf[b, ln] = kn_ref[b]
            vbuf[b, ln] = vn_ref[b]
        for g in range(group):
            b = i * group + g
            ln = len_ref[y * rows + b]
            qw = q_ref[b].astype(F32)
            a = (qw + u_ref[layer].astype(F32)).astype(BF)
            c = (qw + w_ref[layer].astype(F32)).astype(BF)
            lhs = jnp.concatenate([a, c], axis=1)
            kk = kbuf[b].reshape(span, hd)
            rr = rext[pl.ds(seq - 1 - ln, seq)].reshape(span, hd)
            rhs = jnp.concatenate([kk, rr], axis=1)
            s = lax.dot_general(lhs, rhs, (((1,), (1,)), ((), ())), preferred_element_type=F32)
            s = jnp.where(own & (pos <= ln), s * scale, -1e30)
            m = jnp.max(s, axis=1, keepdims=True)
            e = jnp.exp(s - m)
            p = (e / jnp.sum(e, axis=1, keepdims=True)).astype(BF)
            o = jnp.dot(p, vbuf[b].reshape(span, hd), preferred_element_type=F32)
            ctx_ref[b] = o.astype(BF)
        for c in save(i):
            c.start()

    @pl.loop(0, n_grp)
    def _(i):
        for c in save(i):
            c.wait()


def attend_cache(layer, lengths, q, kn, vn, rel, u, w, kc, vc, prev, group=4):
    rows, seq, heads, hd = kc.shape[1:]
    any_ = pl.BlockSpec(memory_space=pl.ANY)
    vm = pl.BlockSpec(memory_space=pltpu.VMEM)
    n_grp = rows // group
    ins = [lengths, q, kn, vn, rel, u, w, kc, vc]
    specs = [pl.BlockSpec(memory_space=pltpu.SMEM), vm, vm, vm,
             vm, vm, vm, any_, any_]
    alias = {}
    if prev is not None:
        ins += list(prev)
        specs += [any_, any_]
        alias = {9: 1, 10: 2}
    return pl.pallas_call(
        functools.partial(attn_body, layer, group),
        out_shape=(jax.ShapeDtypeStruct((rows, heads, hd), BF), jax.ShapeDtypeStruct(kc.shape, BF), jax.ShapeDtypeStruct(vc.shape, BF)),
        in_specs=specs,
        out_specs=(vm, any_, any_),
        input_output_aliases=alias,
        scratch_shapes=[pltpu.VMEM((rows, seq, heads, hd), BF), pltpu.VMEM((rows, seq, heads, hd), BF),
                        pltpu.VMEM((2 * seq, heads, hd), BF), pltpu.SemaphoreType.DMA((2, n_grp)), pltpu.SemaphoreType.DMA((2, n_grp))],
        compiler_params=pltpu.CompilerParams(vmem_limit_bytes=40 << 20),
        cost_estimate=pl.CostEstimate(flops=2 * 2 * rows * heads * span_of(seq, heads) * hd, bytes_accessed=4 * rows * seq * heads * hd * 2, transcendentals=rows * heads * seq),
        name=f"attend_{layer}",
    )(*ins)


def span_of(seq, heads):
    return seq * heads


def solution(mesh):
    y_size = mesh.shape["y"]
    cache_spec = P(None, ("rep", "y"), None, "x", None)
    row_spec = P("rep", "y")
    proj_spec = P(None, "y", "x", None)
    head_spec = P(None, "x", None)
    in_specs = (row_spec, P("rep"), cache_spec, cache_spec, P(None, None, "x", None), P(None, "y"),
                proj_spec, proj_spec, proj_spec, head_spec, head_spec, P(None, "x", None, "y"),
                P(None, "y"), P(None, "y", "x"), P(None, "x", "y"))
    out_specs = (row_spec, cache_spec, cache_spec)

    def local_step(hidden, lengths, k_cache, v_cache, rel_table, norm_attn, w_q, w_k, w_v, bias_content, bias_pos, w_out, norm_mlp, w_up, w_down):
        rows_local = k_cache.shape[1]
        row_start = lax.axis_index("y") * rows_local
        len_local = lax.dynamic_slice_in_dim(lengths, row_start, rows_local)
        d_total = hidden.shape[1] * y_size
        prev = None
        for layer in range(k_cache.shape[0]):
            normed = sharded_norm(hidden, norm_attn[layer], d_total)
            q_part = jnp.einsum("bd,dhe->bhe", normed, w_q[layer], preferred_element_type=jnp.float32).astype(jnp.bfloat16)
            k_part = jnp.einsum("bd,dhe->bhe", normed, w_k[layer], preferred_element_type=jnp.float32).astype(jnp.bfloat16)
            v_part = jnp.einsum("bd,dhe->bhe", normed, w_v[layer], preferred_element_type=jnp.float32).astype(jnp.bfloat16)
            q_full, k_full, v_full = lax.psum((q_part, k_part, v_part), "y")
            q_rows = lax.dynamic_slice_in_dim(q_full, row_start, rows_local)
            k_rows = lax.dynamic_slice_in_dim(k_full, row_start, rows_local)
            v_rows = lax.dynamic_slice_in_dim(v_full, row_start, rows_local)
            context, k_out, v_out = attend_cache(layer, lengths, q_rows, k_rows, v_rows, rel_table, bias_content, bias_pos, k_cache, v_cache, prev)
            prev = (k_out, v_out)
            context_all = lax.all_gather(context, "y", axis=0, tiled=True)
            attn_part = jnp.einsum("bhe,hed->bd", context_all, w_out[layer], preferred_element_type=jnp.float32).astype(jnp.bfloat16)
            attn_out = lax.psum(attn_part, "x")
            hidden = (hidden.astype(jnp.float32) + attn_out.astype(jnp.float32)).astype(jnp.bfloat16)
            normed = sharded_norm(hidden, norm_mlp[layer], d_total)
            up_part = jnp.dot(normed, w_up[layer], preferred_element_type=jnp.float32).astype(jnp.bfloat16)
            up_proj = lax.psum(up_part, "y")
            activated = jax.nn.gelu(up_proj.astype(jnp.float32), approximate=True).astype(jnp.bfloat16)
            down_part = jnp.dot(activated, w_down[layer], preferred_element_type=jnp.float32).astype(jnp.bfloat16)
            down_out = lax.psum(down_part, "x")
            hidden = (hidden.astype(jnp.float32) + down_out.astype(jnp.float32)).astype(jnp.bfloat16)
        return hidden, prev[0], prev[1]

    return jax.shard_map(local_step, mesh=mesh, in_specs=in_specs, out_specs=out_specs, check_vma=False)
```

time: 398 us -> 360 us (0.905)
  other arithmetic: 103 us -> 7.27 us
  waiting for transfers between devices: 143 us -> 195 us
  Pallas kernels: 0 us -> 37.3 us
  local copies, waits for them, and re-layouts: 35.8 us -> 19.7 us
  matrix products: 64.8 us -> 54.2 us
    pallas_call x0 -> x2, Pallas kernels: none -> 37.3 us  [attend_cache(): pl.pallas_call(functools.partial(attn_body, layer, group), out_shape=(jax...]
    select_n x3 -> x0, other arithmetic: 36.4 us -> none  [write_rows(): jnp.where(hit_mask[:, :, None, None], new_rows[:, None, :, :], cache_layer)]
    another operation x2 -> x0, other arithmetic: 27.7 us -> none  [local_step(): return (hidden, jnp.stack(k_layers), jnp.stack(v_layers))]
    unnamed x6 -> x2, other arithmetic: 24.9 us -> 0.01 us
    psum x2, waiting for transfers between devices: 30.5 us -> 53.4 us  [local_step(): attn_out = lax.psum(attn_part, 'x')]
    psum x2, waiting for transfers between devices: 39.6 us -> 53.5 us  [local_step(): down_out = lax.psum(down_part, 'x')]
    psum x2, waiting for transfers between devices: 32.1 us -> 45.9 us  [local_step(): up_proj = lax.psum(up_part, 'y')]
    gather x2 -> x0, local copies, waits for them, and re-layouts: 9.78 us -> none  [shift_rel(): lax.dynamic_slice_in_dim(rel_row, start_at, seq_len, axis=1)]
  transfers between devices with their start and end apart: 8 -> 8, of which waited for: 8 -> 8; matrix products, arithmetic and copies ran while one was open for 13% -> 0% of each run, Pallas kernels for 0% -> 0%
where the time goes in v1:
time: 360 us; the launch traced here: 359 us
  waiting for transfers between devices  195 us (54%)
  matrix products  54.2 us (15%)
  Pallas kernels  37.3 us (10%)
  blocking collectives  31.1 us (9%)
  local copies, waits for them, and re-layouts  19.7 us (5%)
  between operations  14.4 us (4%)
  other arithmetic  7.27 us (2%)
    psum x2, waiting for transfers between devices, local_step(): down_out = lax.psum(down_part, 'x')  53.5 us
    psum x2, waiting for transfers between devices, local_step(): attn_out = lax.psum(attn_part, 'x')  53.4 us
    psum x2, waiting for transfers between devices, local_step(): up_proj = lax.psum(up_part, 'y')  45.9 us
    psum x2, waiting for transfers between devices, local_step(): q_full, k_full, v_full = lax.psum((q_part, k_part, v_part), 'y')  41.8 us
    pallas_call x2, Pallas kernels, attend_cache(): pl.pallas_call(functools.partial(attn_body, layer, group), out_shape=(jax...  37.3 us
    psum x4, blocking collectives, sharded_norm(): lax.psum(jnp.sum(hidden_wide * hidden_wide, axis=1, keepdims=True), 'y')  21.3 us
    dot_general x2, matrix products, local_step(): jnp.dot(normed, w_up[layer], preferred_element_type=jnp.float32)  19.6 us
    dot_general x2, matrix products, local_step(): jnp.dot(activated, w_down[layer], preferred_element_type=jnp.float32)  19.4 us
  transfers between devices with their start and end apart: 8, of which 8 were waited for; matrix products, arithmetic and copies ran while one was open for 0% of the time, Pallas kernels for 0%

profile of v1, /device:TPU:0, one launch (start us, length us, event | category | flops | bytes accessed | tf_op | source)
XLA Modules:
  0.0 358.9 jit_solution(681308458377460503)
XLA Ops:
  7.2 0.0 all-reduce.25.cloned.1.call-start
  7.2 1.1 fusion.62
  8.3 6.3 %psum.112 = f32[64,1]{0,1:T(1,128)S(1)} all-reduce(f32[64,1]{0,1:T(1,128)S(1)} %bitcast.99), channel_id=1, replica_groups=mesh['rep'=1,'y'=2,'x'=4] {'y'}, use_global_device_ids=true, to_apply=%region_1.0 | all-reduce | flops 64 | bytes 512 | tf_op jit(solution)/shard_map/psum | solution.py:17
  14.6 0.9 slice_convert_fusion.1
  15.5 5.4 %fusion.115 = (bf16[1,2048,8,128]{3,2,1,0:T(8,128)(2,1)S(1)}, bf16[1,2048,8,128]{3,2,1,0:T(8,128)(2,1)}) fusion(bf16[2,2048,8,128]{3,2,1,0:T(8,128)(2,1)} %param.21), kind=kLoop, calls=%fused_computation.132 | loop fusion | bytes 16777216 | tf_op jit(solution)/shard_map/slice | solution.py:141
  20.9 0.9 fusion.23
  21.8 0.7 copy.81
  22.6 2.4 fusion.114
  25.0 0.9 fusion.22
  25.9 0.7 copy.80
  26.7 0.2 slice-done.3
  26.9 2.2 fusion.113
  29.2 0.9 fusion.21
  30.1 0.7 copy.79
  30.8 0.0 all-reduce.25.cloned.1.call-update
  30.8 0.0 all-reduce.11.cloned.1.call-start
  30.9 21.6 %all-reduce.25.cloned.1.call-done = (bf16[64,8,128]{2,1,0:T(8,128)(2,1)}, bf16[64,8,128]{2,1,0:T(8,128)(2,1)}, bf16[64,8,128]{2,1,0:T(8,128)(2,1)}) async-done(((bf16[64,8,128]{2,1,0:T(8,128)(2,1)}, bf16[64,8,128]{2,1,0:T(8,128)(2,1)}, bf16[64,8,128]{2,1,0:T(8,128)(2,1)}), (bf16[64,8,128]{2,1,0:T(8,128)(2,1)}, bf16[64,8,128]{2,1,0:T(8,128)(2,1)}, ...) | async-done | bytes 393232 | tf_op jit(solution)/shard_map/psum | solution.py:144
  52.5 0.8 constant_dynamic-slice_fusion.5.q_ref
  53.4 0.9 constant_dynamic-slice_fusion.3
  54.3 18.7 %attend_0.1 = (bf16[32,8,128]{2,1,0:T(8,128)(2,1)S(1)}, bf16[2,32,128,8,128]{4,3,2,1,0:T(8,128)(2,1)}, bf16[2,32,128,8,128]{4,3,2,1,0:T(8,128)(2,1)}) custom-call(s32[64]{0:T(128)S(1)} %copy-done.3, bf16[32,8,128]{2,1,0:T(8,128)(2,1)S(1)} %constant_dynamic-slice_fusion.5.q_ref, bf16[32,8,128]{2,1,0:T(8,128)(2,1)S(1)} %get-tuple-element.34.kn_ref, ...), custom_call_target="tpu_custom_call" | custom-call | flops 134217728 | bytes 33554432 | tf_op jit(solution)/shard_map/attend_0/pallas_call | solution.py:104
  73.0 4.9 %all_gather.6 = bf16[64,8,128]{2,1,0:T(8,128)(2,1)S(1)} all-gather(bf16[32,8,128]{2,1,0:T(8,128)(2,1)S(1)} %get-tuple-element.9), channel_id=1, replica_groups=mesh['rep'=1,'y'=2,'x'=4] {'y'}, dimensions={0}, use_global_device_ids=true | all-gather | bytes 196608 | tf_op jit(solution)/shard_map/all_gather | solution.py:150
  77.9 3.7 %fusion.39 = bf16[64,2048]{1,0:T(8,128)(2,1)} fusion(bf16[2,8,128,2048]{3,2,1,0:T(8,128)(2,1)} %param.26, bf16[64,8,128]{2,1,0:T(8,128)(2,1)S(1)} %all_gather.6), kind=kOutput, calls=%fused_computation.35 | convolution fusion | flops 268566528 | bytes 4587520 | tf_op jit(solution)/shard_map/bhe,hed->bd/dot_general | solution.py:151
  81.7 0.0 all-reduce.11.cloned.1.call-update
  81.7 0.0 all-reduce.13.cloned.1.call-start
  81.8 26.7 %all-reduce.11.cloned.1.call-done = bf16[64,2048]{1,0:T(8,128)(2,1)} async-done(((bf16[64,2048]{1,0:T(8,128)(2,1)}), bf16[64,2048]{1,0:T(8,128)(2,1)}) %all-reduce.11.cloned.1.call-update) | async-done | bytes 262160 | tf_op jit(solution)/shard_map/psum | solution.py:152
  108.4 1.1 fusion.66
  109.6 4.9 %psum.117 = f32[64,1]{0,1:T(1,128)S(1)} all-reduce(f32[64,1]{0,1:T(1,128)S(1)} %bitcast.100), channel_id=1, replica_groups=mesh['rep'=1,'y'=2,'x'=4] {'y'}, use_global_device_ids=true, to_apply=%region_7.0 | all-reduce | flops 64 | bytes 512 | tf_op jit(solution)/shard_map/psum | solution.py:17
  114.5 9.8 %fusion.12 = bf16[64,4096]{1,0:T(8,128)(2,1)} fusion(bf16[2,2048,4096]{2,1,0:T(8,128)(2,1)} %param.28, f32[2048]{0:T(1024)S(1)} %bitcast.97, f32[64]{0:T(128)S(1)} %rsqrt_bitcast_fusion.2, bf16[64,2048]{1,0:T(8,128)(2,1)S(1)} %copy-done.6, bf16[64,2048]{1,0:T(8,128)(2,1)} %all-reduce.11.cloned.1.call-done), kind=kOutput, calls=%fused_computation.12 | convolution fusion | flops 1075052544 | bytes 17834240 | tf_op jit(solution)/shard_map/dot_general | solution.py:155
  124.4 0.0 all-reduce.15.cloned.1.call-start
  124.4 22.9 %all-reduce.13.cloned.1.call-done = bf16[64,4096]{1,0:T(8,128)(2,1)} async-done(((bf16[64,4096]{1,0:T(8,128)(2,1)}), bf16[64,4096]{1,0:T(8,128)(2,1)}) %all-reduce.13.cloned.1.call-update) | async-done | bytes 524304 | tf_op jit(solution)/shard_map/psum | solution.py:156
  147.4 9.7 %fusion.42 = bf16[64,2048]{1,0:T(8,128)(2,1)} fusion(bf16[2,4096,2048]{2,1,0:T(8,128)(2,1)} %param.29, bf16[64,4096]{1,0:T(8,128)(2,1)} %all-reduce.13.cloned.1.call-done), kind=kOutput, calls=%fused_computation.36 | convolution fusion | flops 1076494336 | bytes 17563648 | tf_op jit(solution)/shard_map/dot_general | solution.py:158
  157.1 0.0 all-reduce.15.cloned.1.call-update
  157.1 0.0 all-reduce.23.cloned.1.call-start
  157.1 26.7 %all-reduce.15.cloned.1.call-done = bf16[64,2048]{1,0:T(8,128)(2,1)} async-done(((bf16[64,2048]{1,0:T(8,128)(2,1)}), bf16[64,2048]{1,0:T(8,128)(2,1)}) %all-reduce.15.cloned.1.call-update) | async-done | bytes 262160 | tf_op jit(solution)/shard_map/psum | solution.py:159
  183.9 1.2 fusion.70
  185.0 5.1 %psum.120 = f32[64,1]{0,1:T(1,128)S(1)} all-reduce(f32[64,1]{0,1:T(1,128)S(1)} %bitcast.98), channel_id=1, replica_groups=mesh['rep'=1,'y'=2,'x'=4] {'y'}, use_global_device_ids=true, to_apply=%region_11.0 | all-reduce | flops 64 | bytes 512 | tf_op jit(solution)/shard_map/psum | solution.py:17
  190.2 3.2 fusion.19
  193.4 0.2 copy-done.5
  193.6 0.9 fusion.18
  194.5 0.4 copy-done.4
  194.9 0.9 fusion.20
  195.8 0.7 copy.78
  196.5 0.7 copy.76
  197.2 0.7 copy.77
  198.0 0.0 all-reduce.23.cloned.1.call-update
  198.0 0.0 all-reduce.17.cloned.1.call-start
  198.1 20.1 %all-reduce.23.cloned.1.call-done = (bf16[64,8,128]{2,1,0:T(8,128)(2,1)}, bf16[64,8,128]{2,1,0:T(8,128)(2,1)}, bf16[64,8,128]{2,1,0:T(8,128)(2,1)}) async-done(((bf16[64,8,128]{2,1,0:T(8,128)(2,1)}, bf16[64,8,128]{2,1,0:T(8,128)(2,1)}, bf16[64,8,128]{2,1,0:T(8,128)(2,1)}), (bf16[64,8,128]{2,1,0:T(8,128)(2,1)}, bf16[64,8,128]{2,1,0:T(8,128)(2,1)}, ...) | async-done | bytes 393232 | tf_op jit(solution)/shard_map/psum | solution.py:144
  218.2 0.8 constant_dynamic-slice_fusion.2.q_ref
  219.0 0.8 constant_dynamic-slice_fusion.1.kn_ref
  219.9 0.8 constant_dynamic-slice_fusion.vn_ref
  220.7 18.7 %attend_1.1 = (bf16[32,8,128]{2,1,0:T(8,128)(2,1)S(1)}, bf16[2,32,128,8,128]{4,3,2,1,0:T(8,128)(2,1)}, bf16[2,32,128,8,128]{4,3,2,1,0:T(8,128)(2,1)}) custom-call(s32[64]{0:T(128)S(1)} %copy-done.3, bf16[32,8,128]{2,1,0:T(8,128)(2,1)S(1)} %constant_dynamic-slice_fusion.2.q_ref, ...), custom_call_target="tpu_custom_call", output_to_operand_aliasing={{1}: (9, {}), {2}: (10, {})} | custom-call | flops 134217728 | bytes 33554432 | tf_op jit(solution)/shard_map/attend_1/pallas_call | solution.py:104
  239.4 4.9 %all_gather.7 = bf16[64,8,128]{2,1,0:T(8,128)(2,1)S(1)} all-gather(bf16[32,8,128]{2,1,0:T(8,128)(2,1)S(1)} %get-tuple-element.12), channel_id=1, replica_groups=mesh['rep'=1,'y'=2,'x'=4] {'y'}, dimensions={0}, use_global_device_ids=true | all-gather | bytes 196608 | tf_op jit(solution)/shard_map/all_gather | solution.py:150
  244.3 3.7 %fusion.36 = bf16[64,2048]{1,0:T(8,128)(2,1)} fusion(bf16[2,8,128,2048]{3,2,1,0:T(8,128)(2,1)} %param.26, bf16[64,8,128]{2,1,0:T(8,128)(2,1)S(1)} %all_gather.7), kind=kOutput, calls=%fused_computation.34 | convolution fusion | flops 268566528 | bytes 4587520 | tf_op jit(solution)/shard_map/bhe,hed->bd/dot_general | solution.py:151
  248.1 0.0 all-reduce.17.cloned.1.call-update
  248.1 0.0 all-reduce.19.cloned.1.call-start
  248.2 26.7 %all-reduce.17.cloned.1.call-done = bf16[64,2048]{1,0:T(8,128)(2,1)} async-done(((bf16[64,2048]{1,0:T(8,128)(2,1)}), bf16[64,2048]{1,0:T(8,128)(2,1)}) %all-reduce.17.cloned.1.call-update) | async-done | bytes 262160 | tf_op jit(solution)/shard_map/psum | solution.py:152
  274.9 1.1 fusion.74
  276.0 4.9 %psum.125 = f32[64,1]{0,1:T(1,128)S(1)} all-reduce(f32[64,1]{0,1:T(1,128)S(1)} %bitcast.101), channel_id=1, replica_groups=mesh['rep'=1,'y'=2,'x'=4] {'y'}, use_global_device_ids=true, to_apply=%region_17.0 | all-reduce | flops 64 | bytes 512 | tf_op jit(solution)/shard_map/psum | solution.py:17
  280.9 9.8 %fusion.15 = bf16[64,4096]{1,0:T(8,128)(2,1)} fusion(bf16[2,2048,4096]{2,1,0:T(8,128)(2,1)} %param.28, f32[2048]{0:T(1024)S(1)} %bitcast.93, f32[64]{0:T(128)S(1)} %rsqrt_bitcast_fusion, bf16[64,2048]{1,0:T(8,128)(2,1)S(1)} %get-tuple-element.22, bf16[64,2048]{1,0:T(8,128)(2,1)} %all-reduce.17.cloned.1.call-done), kind=kOutput, calls=%fused_computation.13 | convolution fusion | flops 1075052544 | bytes 17834240 | tf_op jit(solution)/shard_map/dot_general | solution.py:155
  290.8 0.0 all-reduce.21.cloned.1.call-start
  290.8 22.9 %all-reduce.19.cloned.1.call-done = bf16[64,4096]{1,0:T(8,128)(2,1)} async-done(((bf16[64,4096]{1,0:T(8,128)(2,1)}), bf16[64,4096]{1,0:T(8,128)(2,1)}) %all-reduce.19.cloned.1.call-update) | async-done | bytes 524304 | tf_op jit(solution)/shard_map/psum | solution.py:156
  313.8 9.7 %fusion.45 = bf16[64,2048]{1,0:T(8,128)(2,1)} fusion(bf16[2,4096,2048]{2,1,0:T(8,128)(2,1)} %param.29, bf16[64,4096]{1,0:T(8,128)(2,1)} %all-reduce.19.cloned.1.call-done), kind=kOutput, calls=%fused_computation.37 | convolution fusion | flops 1076494336 | bytes 17563648 | tf_op jit(solution)/shard_map/dot_general | solution.py:158
  323.5 26.8 %all-reduce.21.cloned.1.call-done = bf16[64,2048]{1,0:T(8,128)(2,1)} async-done(((bf16[64,2048]{1,0:T(8,128)(2,1)}), bf16[64,2048]{1,0:T(8,128)(2,1)}) %all-reduce.21.cloned.1.call-update) | async-done | bytes 262160 | tf_op jit(solution)/shard_map/psum | solution.py:159
  350.3 1.8 fusion.77
  (35 shorter events, 0.2 us)
Async XLA Ops:
  7.2 45.4 %all-reduce.25.cloned.1.call-start = ((), (), s32[]{:S(2)}) async-start(), calls=%async_computation.7 | async-start | bytes 786432 | tf_op jit(solution)/shard_map/psum | solution.py:144
  14.6 8.0 %slice-start = ((s8[8388608]{0:T(1024)(128)(4,1)}), s8[4194304]{0:T(1024)(128)(4,1)S(1)}, s32[]{:S(2)}) async-start(s8[8388608]{0:T(1024)(128)(4,1)} %bitcast.86), calls=%async_computation.8 | async-start | bytes 8388608
  15.5 5.4 %copy-start.6 = (bf16[64,2048]{1,0:T(8,128)(2,1)S(1)}, bf16[64,2048]{1,0:T(8,128)(2,1)}, u32[]{:S(2)}) copy-start(bf16[64,2048]{1,0:T(8,128)(2,1)} %param.15) | copy-start | bytes 786436
  15.5 7.1 %slice-start.1 = ((s8[8388608]{0:T(1024)(128)(4,1)}), s8[4194304]{0:T(1024)(128)(4,1)S(1)}, s32[]{:S(2)}) async-start(s8[8388608]{0:T(1024)(128)(4,1)} %bitcast.86), calls=%async_computation.9 | async-start | bytes 8388608
  21.8 4.8 %slice-start.2 = ((s8[8388608]{0:T(1024)(128)(4,1)}), s8[4194304]{0:T(1024)(128)(4,1)S(1)}, s32[]{:S(2)}) async-start(s8[8388608]{0:T(1024)(128)(4,1)} %bitcast.88), calls=%async_computation.10 | async-start | bytes 8388608
  22.6 4.3 %slice-start.3 = ((s8[8388608]{0:T(1024)(128)(4,1)}), s8[4194304]{0:T(1024)(128)(4,1)S(1)}, s32[]{:S(2)}) async-start(s8[8388608]{0:T(1024)(128)(4,1)} %bitcast.88), calls=%async_computation.11 | async-start | bytes 8388608
  29.2 25.1 %copy-start = (bf16[2,128,8,128]{3,2,1,0:T(8,128)(2,1)S(1)}, bf16[2,128,8,128]{3,2,1,0:T(8,128)(2,1)}, u32[]{:S(2)}) copy-start(bf16[2,128,8,128]{3,2,1,0:T(8,128)(2,1)} %rel_ref.3) | copy-start | bytes 1572868
  29.2 25.1 %copy-start.1 = (bf16[2,8,128]{2,1,0:T(8,128)(2,1)S(1)}, bf16[2,8,128]{2,1,0:T(8,128)(2,1)}, u32[]{:S(2)}) copy-start(bf16[2,8,128]{2,1,0:T(8,128)(2,1)} %u_ref.3) | copy-start | bytes 12292
  29.2 25.1 %copy-start.2 = (bf16[2,8,128]{2,1,0:T(8,128)(2,1)S(1)}, bf16[2,8,128]{2,1,0:T(8,128)(2,1)}, u32[]{:S(2)}) copy-start(bf16[2,8,128]{2,1,0:T(8,128)(2,1)} %w_ref.3) | copy-start | bytes 12292
  29.2 25.1 %copy-start.3 = (s32[64]{0:T(128)S(1)}, s32[64]{0:T(128)}, u32[]{:S(2)}) copy-start(s32[64]{0:T(128)} %len_ref.3) | copy-start | bytes 772
  30.8 77.6 %all-reduce.11.cloned.1.call-start = ((), (), s32[]{:S(2)}) async-start(), calls=%async_computation | async-start | bytes 524288 | tf_op jit(solution)/shard_map/psum | solution.py:152
  73.0 8.8 %copy-start.9 = (bf16[2,2048]{1,0:T(2,128)(2,1)S(1)}, bf16[2,2048]{1,0:T(2,128)(2,1)}, u32[]{:S(2)}) copy-start(bf16[2,2048]{1,0:T(2,128)(2,1)} %param.27) | copy-start | bytes 24580
  81.7 65.7 %all-reduce.13.cloned.1.call-start = ((), (), s32[]{:S(2)}) async-start(), calls=%async_computation.1 | async-start | bytes 1048576 | tf_op jit(solution)/shard_map/psum | solution.py:156
  124.4 59.5 %copy-start.7 = (bf16[64,2048]{1,0:T(8,128)(2,1)S(1)}, bf16[64,2048]{1,0:T(8,128)(2,1)}, u32[]{:S(2)}) copy-start(bf16[64,2048]{1,0:T(8,128)(2,1)} %all-reduce.11.cloned.1.call-done) | copy-start | bytes 786436
  124.4 59.5 %all-reduce.15.cloned.1.call-start = ((), (), s32[]{:S(2)}) async-start(), calls=%async_computation.2 | async-start | bytes 524288 | tf_op jit(solution)/shard_map/psum | solution.py:159
  157.1 61.1 %all-reduce.23.cloned.1.call-start = ((), (), s32[]{:S(2)}) async-start(), calls=%async_computation.6 | async-start | bytes 786432 | tf_op jit(solution)/shard_map/psum | solution.py:144
  190.2 3.4 copy-start.5
  190.2 4.7 %copy-start.4 = (bf16[1,2048,8,128]{3,2,1,0:T(8,128)(2,1)S(1)}, bf16[1,2048,8,128]{3,2,1,0:T(8,128)(2,1)}, u32[]{:S(2)}) copy-start(bf16[1,2048,8,128]{3,2,1,0:T(8,128)(2,1)} %get-tuple-element.28) | copy-start | bytes 12582916
  198.0 76.8 %all-reduce.17.cloned.1.call-start = ((), (), s32[]{:S(2)}) async-start(), calls=%async_computation.3 | async-start | bytes 524288 | tf_op jit(solution)/shard_map/psum | solution.py:152
  248.1 65.7 %all-reduce.19.cloned.1.call-start = ((), (), s32[]{:S(2)}) async-start(), calls=%async_computation.4 | async-start | bytes 1048576 | tf_op jit(solution)/shard_map/psum | solution.py:156
  290.8 59.5 %copy-start.8 = (bf16[64,2048]{1,0:T(8,128)(2,1)S(1)}, bf16[64,2048]{1,0:T(8,128)(2,1)}, u32[]{:S(2)}) copy-start(bf16[64,2048]{1,0:T(8,128)(2,1)} %all-reduce.17.cloned.1.call-done) | copy-start | bytes 786436
  290.8 59.5 %all-reduce.21.cloned.1.call-start = ((), (), s32[]{:S(2)}) async-start(), calls=%async_computation.5 | async-start | bytes 524288 | tf_op jit(solution)/shard_map/psum | solution.py:159
Sparse Core Ops, SparseCore 0:
  31.0 21.5 all-reduce.24
  81.8 26.5 all-reduce.10
  124.5 22.8 all-reduce.12
  157.2 26.6 all-reduce.14
  198.1 20.0 all-reduce.22
  248.2 26.5 all-reduce.16
  290.9 22.8 all-reduce.18
  323.6 26.5 all-reduce.20

commit v2 on v1

--- a/solution.py
+++ b/solution.py
@@ -8,16 +8,6 @@
 
 BF = jnp.bfloat16
 F32 = jnp.float32
-
-EPS = 1e-6
-
-
-def sharded_norm(hidden, gain, d_total):
-    hidden_wide = hidden.astype(jnp.float32)
-    sum_sq = lax.psum(jnp.sum(hidden_wide * hidden_wide, axis=1, keepdims=True), "y")
-    inv_rms = lax.rsqrt(sum_sq / d_total + EPS)
-    return (hidden_wide * inv_rms * gain.astype(jnp.float32)).astype(jnp.bfloat16)
-
 
 def attn_body(layer, group, len_ref, q_ref, kn_ref, vn_ref, rel_ref, u_ref, w_ref, kc, vc, *rest):
     ctx_ref, ko, vo, kbuf, vbuf, rext, rsem, wsem = rest[-8:]
@@ -60,8 +50,8 @@
         for g in range(group):
             b = i * group + g
             ln = len_ref[y * rows + b]
-            kbuf[b, ln] = kn_ref[b]
-            vbuf[b, ln] = vn_ref[b]
+            kbuf[b, ln] = kn_ref[b].astype(BF)
+            vbuf[b, ln] = vn_ref[b].astype(BF)
         for g in range(group):
             b = i * group + g
             ln = len_ref[y * rows + b]
@@ -78,7 +68,7 @@
             e = jnp.exp(s - m)
             p = (e / jnp.sum(e, axis=1, keepdims=True)).astype(BF)
             o = jnp.dot(p, vbuf[b].reshape(span, hd), preferred_element_type=F32)
-            ctx_ref[b] = o.astype(BF)
+            ctx_ref[b] = o.astype(BF).astype(F32)
         for c in save(i):
             c.start()
 
@@ -103,7 +93,7 @@
         alias = {9: 1, 10: 2}
     return pl.pallas_call(
         functools.partial(attn_body, layer, group),
-        out_shape=(jax.ShapeDtypeStruct((rows, heads, hd), BF), jax.ShapeDtypeStruct(kc.shape, BF), jax.ShapeDtypeStruct(vc.shape, BF)),
+        out_shape=(jax.ShapeDtypeStruct((rows, heads, hd), F32), jax.ShapeDtypeStruct(kc.shape, BF), jax.ShapeDtypeStruct(vc.shape, BF)),
         in_specs=specs,
         out_specs=(vm, any_, any_),
         input_output_aliases=alias,
@@ -119,8 +109,252 @@
     return seq * heads
 
 
+MESH = pl.DeviceIdType.MESH
+EPS = 1e-6
+UP_CHUNK = 512
+DIM_NT = (((1,), (1,)), ((), ()))
+
+
+def rows_to_cols(col):
+    square = jnp.concatenate([col] * (128 // col.shape[0]), axis=0)
+    return jnp.broadcast_to(jnp.sum(square.T, axis=0, keepdims=True), (8, 128))
+
+
+def cols_to_rows(row, n):
+    return jnp.broadcast_to(row[0:1], (128, 128)).T[:n, 0:1]
+
+
+def stage_body(pre, qkv, layer, names, *refs):
+    r = dict(zip(names, refs))
+    batch, width = r["hidden"].shape
+    half = width // 2
+    rows = batch // 2
+    x = lax.axis_index("x")
+    y = lax.axis_index("y")
+    y_dev = {"y": 1 - y}
+    core = x % 2
+    pair_dev = {"x": x + 1 - 2 * core}
+    chip_dev = {"x": (x + 2) % 4}
+    qkv_layer = layer + 1 if pre else layer
+
+    def remote(src, dst, sems, idx, dev):
+        return pltpu.make_async_remote_copy(src, dst, r[sems].at[0, idx], r[sems].at[1, idx], device_id=dev, device_id_type=MESH)
+
+    def wo_copy(i):
+        n = r["wo"].shape[0] // 4
+        return pltpu.make_async_copy(r["w_out"].at[layer, pl.ds(i * n, n)], r["wo"].at[pl.ds(i * n, n)], r["wo_sem"].at[i])
+
+    def up_copy(i):
+        cols = pl.ds(pl.multiple_of(i * UP_CHUNK, UP_CHUNK), UP_CHUNK)
+        return pltpu.make_async_copy(r["w_up"].at[layer, :, cols], r["wup"].at[:, cols], r["wup_sem"].at[i])
+
+    def down_copy(i):
+        sl = pl.ds(i * UP_CHUNK, UP_CHUNK)
+        return pltpu.make_async_copy(r["w_down"].at[layer, sl], r["wdn"].at[sl], r["wdn_sem"].at[i])
+
+    def qkv_copy(m, i):
+        sl = pl.ds(i * 512, 512)
+        return pltpu.make_async_copy(r[("w_q", "w_k", "w_v")[m]].at[qkv_layer, sl], r["wqkv"].at[m, sl], r["wqkv_sem"].at[m, i])
+
+    k_chunks = width // 512
+
+    def start_qkv():
+        for m in range(3):
+            for i in range(k_chunks):
+                qkv_copy(m, i).start()
+
+    if pre:
+        n_up = r["wup"].shape[1] // UP_CHUNK
+        for i in range(4):
+            wo_copy(i).start()
+
+        @pl.loop(0, n_up)
+        def _(i):
+            up_copy(i).start()
+    else:
+        start_qkv()
+
+    barrier = pltpu.get_barrier_semaphore()
+    greet = [y_dev, pair_dev, chip_dev] if pre else [y_dev]
+    for dev in greet:
+        pl.semaphore_signal(barrier, inc=1, device_id=dev, device_id_type=MESH)
+    pl.semaphore_wait(barrier, len(greet))
+
+    def norm(x_ref, gain_ref, gain_layer, slot):
+        wide = x_ref[...].astype(F32)
+        sq = wide * wide
+        part = sq[:, 0:128]
+        for j in range(1, width // 128):
+            part = part + sq[:, j * 128:(j + 1) * 128]
+        r["ss_send"][slot] = rows_to_cols(part)
+        cp = remote(r["ss_send"].at[slot], r["ss_recv"].at[slot], "ss_sem", slot, y_dev)
+        cp.start()
+        cp.wait()
+        total = cols_to_rows(r["ss_send"][slot] + r["ss_recv"][slot], batch)
+        inv = lax.rsqrt(total / (2 * width) + EPS)
+        gain = gain_ref[pl.ds(gain_layer, 1)].astype(F32)
+        r["h"][...] = (x_ref[...].astype(F32) * inv * gain).astype(BF)
+
+    own = pl.ds(pl.multiple_of(core * half, half), half)
+    other = pl.ds(pl.multiple_of((1 - core) * half, half), half)
+
+    def reduce_x(slot, part_of, x_ref, out_ref):
+        r["pair_send"][slot] = part_of(other).astype(BF)
+        to_pair = remote(r["pair_send"].at[slot], r["pair_recv"].at[slot], "pair_sem", slot, pair_dev)
+        to_pair.start()
+        r["part"][...] = part_of(own)
+        to_pair.wait()
+        r["chip_send"][slot] = (r["part"][...] + r["pair_recv"][slot].astype(F32)).astype(BF)
+        to_chip = remote(r["chip_send"].at[slot], r["chip_recv"].at[slot], "chip_sem", slot, chip_dev)
+        to_chip.start()
+        to_chip.wait()
+        total = r["chip_send"][slot].astype(F32) + r["chip_recv"][slot].astype(F32)
+        out_ref[:, own] = (x_ref[:, own].astype(F32) + total).astype(BF)
+        share = remote(out_ref.at[:, own], out_ref.at[:, own], "share_sem", slot, pair_dev)
+        share.start()
+        share.wait()
+
+    x_now = r["hidden"]
+    if pre:
+        mine = pl.ds(pl.multiple_of(y * rows, rows), rows)
+        heads, hd = r["ctx"].shape[1:]
+        for hh in range(heads):
+            r["ctx_all"][mine, hh * hd:(hh + 1) * hd] = r["ctx"][:, hh, :].astype(BF)
+        cp = remote(r["ctx_all"].at[mine], r["ctx_all"].at[mine], "ctx_sem", 0, y_dev)
+        cp.start()
+        for i in range(4):
+            wo_copy(i).wait()
+        cp.wait()
+
+        def wo_part(cols):
+            return jnp.dot(r["ctx_all"][...], r["wo"][:, cols], preferred_element_type=F32)
+
+        reduce_x(0, wo_part, r["hidden"], r["x_mid"])
+
+        @pl.loop(0, n_up)
+        def _(i):
+            down_copy(i).start()
+        if qkv:
+            start_qkv()
+
+        norm(r["x_mid"], r["g_mlp"], layer, 0)
+
+        def exchange_up(i):
+            cols = pl.ds(pl.multiple_of(i * UP_CHUNK, UP_CHUNK), UP_CHUNK)
+            return remote(r["up_send"].at[:, cols], r["up_recv"].at[:, cols], "up_sem", i, y_dev)
+
+        @pl.loop(0, n_up)
+        def _(i):
+            up_copy(i).wait()
+            cols = pl.ds(pl.multiple_of(i * UP_CHUNK, UP_CHUNK), UP_CHUNK)
+            r["up_send"][:, cols] = jnp.dot(r["h"][...], r["wup"][:, cols], preferred_element_type=F32).astype(BF)
+            exchange_up(i).start()
+
+        def activate(i):
+            cols = pl.ds(pl.multiple_of(i * UP_CHUNK, UP_CHUNK), UP_CHUNK)
+            exchange_up(i).wait()
+            m = (r["up_send"][:, cols].astype(F32) + r["up_recv"][:, cols].astype(F32)).astype(BF)
+            r["act"][...] = jax.nn.gelu(m.astype(F32), approximate=True).astype(BF)
+
+        r["acc"][...] = jnp.zeros_like(r["acc"])
+
+        @pl.loop(0, n_up - 1)
+        def _(i):
+            down_copy(i).wait()
+            activate(i)
+            sl = pl.ds(pl.multiple_of(i * UP_CHUNK, UP_CHUNK), UP_CHUNK)
+            r["acc"][...] += jnp.dot(r["act"][...], r["wdn"][sl, :], preferred_element_type=F32)
+
+        down_copy(n_up - 1).wait()
+        activate(n_up - 1)
+
+        def down_part(cols):
+            last = jnp.dot(r["act"][...], r["wdn"][pl.ds((n_up - 1) * UP_CHUNK, UP_CHUNK), cols], preferred_element_type=F32)
+            return r["acc"][:, cols] + last
+
+        reduce_x(1, down_part, r["x_mid"], r["x_end"])
+        r["x_out"][...] = r["x_end"][...]
+        x_now = r["x_end"]
+
+    if qkv:
+        norm(x_now, r["g_attn"], qkv_layer, 1)
+        heads, hd = r["wqkv"].shape[2:]
+        mine = pl.ds(pl.multiple_of(y * rows, rows), rows)
+        theirs = pl.ds(pl.multiple_of((1 - y) * rows, rows), rows)
+
+        def swap(m):
+            return remote(r["qkv_send"].at[m], r["qkv_recv"].at[m], "qkv_sem", m, y_dev)
+
+        for m in range(3):
+            for i in range(k_chunks):
+                qkv_copy(m, i).wait()
+            r["part"][...] = jnp.zeros_like(r["part"])
+
+            @pl.loop(0, k_chunks)
+            def _(i):
+                sl = pl.ds(pl.multiple_of(i * 512, 512), 512)
+                by_head = jnp.swapaxes(r["wqkv"][m, sl], 0, 1)
+                flat = jnp.concatenate([by_head[hh] for hh in range(heads)], axis=1)
+                r["part"][...] += jnp.dot(r["h"][:, sl], flat, preferred_element_type=F32)
+
+            r["qkv_send"][m] = r["part"][theirs, :].astype(BF)
+            swap(m).start()
+            r["qkv_own"][m] = r["part"][mine, :].astype(BF)
+
+        for m in range(3):
+            swap(m).wait()
+            full = (r["qkv_own"][m].astype(F32) + r["qkv_recv"][m].astype(F32)).astype(BF).astype(F32)
+            out = r[("q", "k", "v")[m]]
+            for hh in range(heads):
+                out[:, hh, :] = full[:, hh * hd:(hh + 1) * hd]
+
+
+def stage(pre, qkv, layer, hidden, ctx, w):
+    batch, width = hidden.shape
+    heads, hd = w["w_q"].shape[2:]
+    rows, half, flat = batch // 2, width // 2, heads * hd
+    ff = w["w_up"].shape[2]
+    n_up = ff // UP_CHUNK
+    vm = pl.BlockSpec(memory_space=pltpu.VMEM)
+    any_ = pl.BlockSpec(memory_space=pl.ANY)
+    dma = pltpu.SemaphoreType.DMA
+    ins = [("hidden", hidden, vm)]
+    outs = []
+    scratch = [("ss_send", pltpu.VMEM((2, 8, 128), F32)), ("ss_recv", pltpu.VMEM((2, 8, 128), F32)), ("ss_sem", dma((2, 2))),
+               ("h", pltpu.VMEM((batch, width), BF)), ("part", pltpu.VMEM((batch, half), F32))]
+    if pre:
+        ins += [("ctx", ctx, vm), ("g_mlp", w["norm_mlp"], vm), ("w_out", w["w_out"], any_), ("w_up", w["w_up"], any_), ("w_down", w["w_down"], any_)]
+        outs += [("x_out", (batch, width), BF)]
+        piece = pltpu.VMEM((2, batch, half), BF)
+        scratch += [("wo", pltpu.VMEM((flat, width), BF)), ("wo_sem", dma((4,))),
+                    ("wup", pltpu.VMEM((width, ff), BF)), ("wup_sem", dma((n_up,))),
+                    ("wdn", pltpu.VMEM((ff, width), BF)), ("wdn_sem", dma((n_up,))),
+                    ("pair_send", piece), ("pair_recv", piece), ("pair_sem", dma((2, 2))),
+                    ("chip_send", piece), ("chip_recv", piece), ("chip_sem", dma((2, 2))), ("share_sem", dma((2, 2))),
+                    ("ctx_all", pltpu.VMEM((batch, flat), BF)), ("ctx_sem", dma((2, 1))),
+                    ("x_mid", pltpu.VMEM((batch, width), BF)), ("x_end", pltpu.VMEM((batch, width), BF)),
+                    ("up_send", pltpu.VMEM((batch, ff), BF)), ("up_recv", pltpu.VMEM((batch, ff), BF)), ("up_sem", dma((2, n_up))),
+                    ("act", pltpu.VMEM((batch, UP_CHUNK), BF)), ("acc", pltpu.VMEM((batch, width), F32))]
+    if qkv:
+        ins += [("g_attn", w["norm_attn"], vm), ("w_q", w["w_q"], any_), ("w_k", w["w_k"], any_), ("w_v", w["w_v"], any_)]
+        outs += [(n, (rows, heads, hd), F32) for n in ("q", "k", "v")]
+        share = pltpu.VMEM((3, rows, flat), BF)
+        scratch += [("wqkv", pltpu.VMEM((3, width, heads, hd), BF)), ("wqkv_sem", dma((3, width // 512))),
+                    ("qkv_send", share), ("qkv_recv", share), ("qkv_own", share), ("qkv_sem", dma((2, 3)))]
+    names = [n for n, *_ in ins] + [n for n, *_ in outs] + [n for n, _ in scratch]
+    return pl.pallas_call(
+        functools.partial(stage_body, pre, qkv, layer, names),
+        out_shape=tuple(jax.ShapeDtypeStruct(s, d) for _, s, d in outs),
+        in_specs=[s for *_, s in ins],
+        out_specs=tuple(vm for _ in outs),
+        scratch_shapes=[s for _, s in scratch],
+        compiler_params=pltpu.CompilerParams(collective_id=(1 if pre else 0) + (2 if qkv else 0), has_side_effects=True,
+                                             vmem_limit_bytes=62 << 20),
+        name=f"stage_{int(pre)}{int(qkv)}",
+    )(*[a for _, a, _ in ins])
+
+
 def solution(mesh):
-    y_size = mesh.shape["y"]
     cache_spec = P(None, ("rep", "y"), None, "x", None)
     row_spec = P("rep", "y")
     proj_spec = P(None, "y", "x", None)
@@ -131,33 +365,17 @@
     out_specs = (row_spec, cache_spec, cache_spec)
 
     def local_step(hidden, lengths, k_cache, v_cache, rel_table, norm_attn, w_q, w_k, w_v, bias_content, bias_pos, w_out, norm_mlp, w_up, w_down):
-        rows_local = k_cache.shape[1]
-        row_start = lax.axis_index("y") * rows_local
-        len_local = lax.dynamic_slice_in_dim(lengths, row_start, rows_local)
-        d_total = hidden.shape[1] * y_size
+        w = dict(norm_attn=norm_attn, w_q=w_q, w_k=w_k, w_v=w_v, norm_mlp=norm_mlp, w_up=w_up, w_down=w_down,
+                 w_out=w_out.reshape(w_out.shape[0], -1, w_out.shape[3]))
+        layers = k_cache.shape[0]
+        q, k, v = stage(False, True, 0, hidden, None, w)
         prev = None
-        for layer in range(k_cache.shape[0]):
-            normed = sharded_norm(hidden, norm_attn[layer], d_total)
-            q_part = jnp.einsum("bd,dhe->bhe", normed, w_q[layer], preferred_element_type=jnp.float32).astype(jnp.bfloat16)
-            k_part = jnp.einsum("bd,dhe->bhe", normed, w_k[layer], preferred_element_type=jnp.float32).astype(jnp.bfloat16)
-            v_part = jnp.einsum("bd,dhe->bhe", normed, w_v[layer], preferred_element_type=jnp.float32).astype(jnp.bfloat16)
-            q_full, k_full, v_full = lax.psum((q_part, k_part, v_part), "y")
-            q_rows = lax.dynamic_slice_in_dim(q_full, row_start, rows_local)
-            k_rows = lax.dynamic_slice_in_dim(k_full, row_start, rows_local)
-            v_rows = lax.dynamic_slice_in_dim(v_full, row_start, rows_local)
-            context, k_out, v_out = attend_cache(layer, lengths, q_rows, k_rows, v_rows, rel_table, bias_content, bias_pos, k_cache, v_cache, prev)
-            prev = (k_out, v_out)
-            context_all = lax.all_gather(context, "y", axis=0, tiled=True)
-            attn_part = jnp.einsum("bhe,hed->bd", context_all, w_out[layer], preferred_element_type=jnp.float32).astype(jnp.bfloat16)
-            attn_out = lax.psum(attn_part, "x")
-            hidden = (hidden.astype(jnp.float32) + attn_out.astype(jnp.float32)).astype(jnp.bfloat16)
-            normed = sharded_norm(hidden, norm_mlp[layer], d_total)
-            up_part = jnp.dot(normed, w_up[layer], preferred_element_type=jnp.float32).astype(jnp.bfloat16)
-            up_proj = lax.psum(up_part, "y")
-            activated = jax.nn.gelu(up_proj.astype(jnp.float32), approximate=True).astype(jnp.bfloat16)
-            down_part = jnp.dot(activated, w_down[layer], preferred_element_type=jnp.float32).astype(jnp.bfloat16)
-            down_out = lax.psum(down_part, "x")
-            hidden = (hidden.astype(jnp.float32) + down_out.astype(jnp.float32)).astype(jnp.bfloat16)
+        for layer in range(layers):
+            ctx, *prev = attend_cache(layer, lengths, q, k, v, rel_table, bias_content, bias_pos, k_cache, v_cache, prev)
+            if layer + 1 < layers:
+                hidden, q, k, v = stage(True, True, layer, hidden, ctx, w)
+            else:
+                hidden, = stage(True, False, layer, hidden, ctx, w)
         return hidden, prev[0], prev[1]
 
     return jax.shard_map(local_step, mesh=mesh, in_specs=in_specs, out_specs=out_specs, check_vma=False)

time: 360 us -> 152 us (0.42)
  waiting for transfers between devices: 195 us -> 0 us
  Pallas kernels: 37.3 us -> 143 us
  matrix products: 54.2 us -> 0 us
  blocking collectives: 31.1 us -> 0 us
  between operations: 14.4 us -> 0.77 us
  local copies, waits for them, and re-layouts: 19.7 us -> 8.4 us
  other arithmetic: 7.27 us -> 0 us
    psum x8 -> x0, waiting for transfers between devices: 194 us -> none  [the longest x2 53.5 us: local_step(): down_out = lax.psum(down_part, 'x')]
    pallas_call x0 -> x3, Pallas kernels: none -> 105 us  [stage(): pl.pallas_call(functools.partial(stage_body, pre, qkv, layer, names), out...]
    dot_general x12 -> x0, matrix products: 54.2 us -> none  [the longest x2 19.6 us: local_step(): jnp.dot(normed, w_up[layer], preferred_element_type=jnp.float32)]
    psum x4 -> x0, blocking collectives: 21.3 us -> none  [sharded_norm(): lax.psum(jnp.sum(hidden_wide * hidden_wide, axis=1, keepdims=True), 'y')]
    slice x3 -> x0, local copies, waits for them, and re-layouts: 10.1 us -> none  [the longest x1 5.42 us: local_step(): w_q[layer]]
    all_gather x2 -> x0, blocking collectives: 9.87 us -> none  [local_step(): context_all = lax.all_gather(context, 'y', axis=0, tiled=True)]
    unnamed x28 -> x25, local copies, waits for them, and re-layouts: 0.89 us -> 8.4 us
    reduce_sum x4 -> x0, other arithmetic: 4.56 us -> none  [sharded_norm(): jnp.sum(hidden_wide * hidden_wide, axis=1, keepdims=True)]
  transfers between devices with their start and end apart: 8 -> 0, of which waited for: 8 -> 0; matrix products, arithmetic and copies ran while one was open for 0% -> 0% of each run, Pallas kernels for 0% -> 0%
where the time goes in v2:
time: 152 us
  Pallas kernels  143 us (94%)
  local copies, waits for them, and re-layouts  8.4 us (6%)
    pallas_call x3, Pallas kernels, stage(): pl.pallas_call(functools.partial(stage_body, pre, qkv, layer, names), out...  105 us
    pallas_call x2, Pallas kernels, attend_cache(): pl.pallas_call(functools.partial(attn_body, layer, group), out_shape=(jax...  37.4 us
    unnamed x25, local copies, waits for them, and re-layouts  8.4 us

profile of v2, /device:TPU:0, one launch (start us, length us, event | category | flops | bytes accessed | tf_op | source)
XLA Modules:
  0.0 151.7 jit_solution(9221311976928197511)
XLA Ops:
  0.6 0.0 copy-start.10
  0.6 0.0 copy-start.9
  0.7 0.0 copy-start
  0.7 0.0 copy-start.11
  0.7 17.5 %stage_01.1 = (f32[32,8,128]{2,1,0:T(8,128)}, f32[32,8,128]{2,1,0:T(8,128)}, f32[32,8,128]{2,1,0:T(8,128)}) custom-call(bf16[64,2048]{1,0:T(8,128)(2,1)} %refs_0_.3, bf16[2,2048]{1,0:T(2,128)(2,1)} %refs_6_.1, bf16[2,2048,8,128]{3,2,1,0:T(8,128)(2,1)} %refs_7_.1, bf16[2,2048,8,128]{3,2,1,0:T(8,128)(2,1)} %refs_8_.1, bf16[2,2048,8,128]{3,2,1,0:T(8,128)(2,1)} %refs_9_.1), custom_call_target="tpu_custom_call" | custom-call | tf_op jit(solution)/shard_map/stage_01/pallas_call | solution.py:345
  18.2 0.0 copy-done.10
  18.2 0.0 copy-done.9
  18.2 0.0 copy-done
  18.2 0.0 copy-done.11
  18.2 0.0 copy-start.6
  18.2 0.9 copy-done.6
  19.1 0.0 copy-start.7
  19.1 0.9 copy-done.7
  20.0 0.0 copy-start.8
  20.0 0.9 copy-done.8
  20.9 18.7 %attend_0.1 = (f32[32,8,128]{2,1,0:T(8,128)S(1)}, bf16[2,32,128,8,128]{4,3,2,1,0:T(8,128)(2,1)}, bf16[2,32,128,8,128]{4,3,2,1,0:T(8,128)(2,1)}) custom-call(s32[64]{0:T(128)S(1)} %copy-done.11, f32[32,8,128]{2,1,0:T(8,128)S(1)} %copy-done.6, f32[32,8,128]{2,1,0:T(8,128)S(1)} %copy-done.7, f32[32,8,128]{2,1,0:T(8,128)S(1)} %copy-done.8, ...), custom_call_target="tpu_custom_call" | custom-call | flops 134217728 | bytes 33554432 | tf_op jit(solution)/shard_map/attend_0/pallas_call | solution.py:94
  39.6 0.0 copy-start.1
  39.6 0.6 copy-done.1
  40.3 50.0 %stage_11.1 = (bf16[64,2048]{1,0:T(8,128)(2,1)}, f32[32,8,128]{2,1,0:T(8,128)}, f32[32,8,128]{2,1,0:T(8,128)}, f32[32,8,128]{2,1,0:T(8,128)}) custom-call(bf16[64,2048]{1,0:T(8,128)(2,1)} %refs_0_.3, f32[32,8,128]{2,1,0:T(8,128)} %copy-done.1, bf16[2,2048]{1,0:T(2,128)(2,1)} %refs_2_.5, bf16[2,1024,2048]{2,1,0:T(8,128)(2,1)} %bitcast.1, ...), custom_call_target="tpu_custom_call" | custom-call | tf_op jit(solution)/shard_map/stage_11/pallas_call | solution.py:345
  90.3 0.0 copy-start.2
  90.3 0.9 copy-done.2
  91.2 0.0 copy-start.3
  91.2 0.9 copy-done.3
  92.1 0.0 copy-start.4
  92.1 0.9 copy-done.4
  93.0 18.7 %attend_1.1 = (f32[32,8,128]{2,1,0:T(8,128)S(1)}, bf16[2,32,128,8,128]{4,3,2,1,0:T(8,128)(2,1)}, bf16[2,32,128,8,128]{4,3,2,1,0:T(8,128)(2,1)}) custom-call(s32[64]{0:T(128)S(1)} %copy-done.11, f32[32,8,128]{2,1,0:T(8,128)S(1)} %copy-done.2, f32[32,8,128]{2,1,0:T(8,128)S(1)} %copy-done.3, ...), custom_call_target="tpu_custom_call", output_to_operand_aliasing={{1}: (9, {}), {2}: (10, {})} | custom-call | flops 134217728 | bytes 33554432 | tf_op jit(solution)/shard_map/attend_1/pallas_call | solution.py:94
  111.7 0.0 copy-start.5
  111.8 0.6 copy-done.5
  112.4 37.6 %stage_10.1 = bf16[64,2048]{1,0:T(8,128)(2,1)} custom-call(bf16[64,2048]{1,0:T(8,128)(2,1)} %get-tuple-element.20.refs_0_, f32[32,8,128]{2,1,0:T(8,128)} %copy-done.5, bf16[2,2048]{1,0:T(2,128)(2,1)} %refs_2_.5, bf16[2,1024,2048]{2,1,0:T(8,128)(2,1)} %bitcast.2, bf16[2,2048,4096]{2,1,0:T(8,128)(2,1)} %refs_4_.5, bf16[2,4096,2048]{2,1,0:T(8,128)(2,1)} %refs_5_.3), custom_call_target="tpu_custom_call" | custom-call | tf_op jit(solution)/shard_map/stage_10/pallas_call | solution.py:345
  150.0 1.7 %copy.23 = bf16[64,2048]{1,0:T(8,128)(2,1)} copy(bf16[64,2048]{1,0:T(8,128)(2,1)} %stage_10.1) | data formatting | bytes 524288
Async XLA Ops:
  0.6 17.5 %copy-start.10 = (bf16[2,8,128]{2,1,0:T(8,128)(2,1)S(1)}, bf16[2,8,128]{2,1,0:T(8,128)(2,1)}, u32[]{:S(2)}) copy-start(bf16[2,8,128]{2,1,0:T(8,128)(2,1)} %w_ref.3) | copy-start | bytes 12292
  0.6 17.5 %copy-start.9 = (bf16[2,8,128]{2,1,0:T(8,128)(2,1)S(1)}, bf16[2,8,128]{2,1,0:T(8,128)(2,1)}, u32[]{:S(2)}) copy-start(bf16[2,8,128]{2,1,0:T(8,128)(2,1)} %u_ref.3) | copy-start | bytes 12292
  0.7 17.5 %copy-start = (bf16[2,128,8,128]{3,2,1,0:T(8,128)(2,1)S(1)}, bf16[2,128,8,128]{3,2,1,0:T(8,128)(2,1)}, u32[]{:S(2)}) copy-start(bf16[2,128,8,128]{3,2,1,0:T(8,128)(2,1)} %rel_ref.3) | copy-start | bytes 1572868
  0.7 17.5 %copy-start.11 = (s32[64]{0:T(128)S(1)}, s32[64]{0:T(128)}, u32[]{:S(2)}) copy-start(s32[64]{0:T(128)} %len_ref.3) | copy-start | bytes 772
  18.2 0.9 copy-start.6
  19.1 0.9 copy-start.7
  20.0 0.9 copy-start.8
  39.6 0.7 copy-start.1
  90.3 0.9 copy-start.2
  91.2 0.9 copy-start.3
  92.1 0.9 copy-start.4
  111.7 0.7 copy-start.5

commit v3 on v2

v3 whole, which is shorter than its diff:
```python
import functools
import jax
import jax.numpy as jnp
from jax import lax
from jax.experimental import pallas as pl
from jax.experimental.pallas import tpu as pltpu
from jax.sharding import PartitionSpec as P

BF = jnp.bfloat16
F32 = jnp.float32

def attn_body(layer, group, len_ref, q_hbm, kn_hbm, vn_hbm, rel_hbm, u_hbm, w_hbm, k_in, v_in, *rest):
    ctx_hbm, ko, vo, kbuf, vbuf, q_ref, kn_ref, vn_ref, rel_ref, u_ref, w_ref, ctx_ref, rext, osem, wsem = rest[-15:]
    rows, span, hd = kbuf.shape
    heads = q_ref.shape[1]
    seq = span // heads
    y = lax.axis_index("y")
    n_grp = rows // group
    small = [(rel_hbm.at[layer], rel_ref), (q_hbm, q_ref), (kn_hbm, kn_ref), (vn_hbm, vn_ref), (u_hbm, u_ref), (w_hbm, w_ref)]
    small = [pltpu.make_async_copy(src, dst, osem.at[i]) for i, (src, dst) in enumerate(small)]
    for c in small:
        c.start()

    def save(i):
        sl = pl.ds(i * group, group)
        return (pltpu.make_async_copy(kbuf.at[sl], ko.at[layer, sl], wsem.at[0, i]),
                pltpu.make_async_copy(vbuf.at[sl], vo.at[layer, sl], wsem.at[1, i]),
                pltpu.make_async_copy(ctx_ref.at[sl], ctx_hbm.at[sl], wsem.at[2, i]))

    @pl.loop(0, seq, unroll=4)
    def _(t):
        rext[pl.ds(pl.multiple_of((seq + t) * heads, heads), heads)] = jnp.zeros((heads, hd), BF)

    small[0].wait()

    @pl.loop(0, seq, unroll=4)
    def _(t):
        rext[pl.ds(pl.multiple_of((seq - 1 - t) * heads, heads), heads)] = rel_ref[t]

    col = lax.broadcasted_iota(jnp.int32, (heads, span), 1)
    row = lax.broadcasted_iota(jnp.int32, (heads, span), 0)
    own = (col % heads) == row
    pos = jnp.where(own, col // heads, 1 << 20)
    scale = hd ** -0.5
    for c in small[1:]:
        c.wait()

    @pl.loop(0, n_grp)
    def _(i):
        for g in range(group):
            b = i * group + g
            ln = len_ref[y * rows + b]
            at = pl.ds(pl.multiple_of(ln * heads, heads), heads)
            kbuf[b, at] = kn_ref[b].astype(BF)
            vbuf[b, at] = vn_ref[b].astype(BF)
        score = []
        for g in range(group):
            b = i * group + g
            ln = len_ref[y * rows + b]
            qw = q_ref[b].astype(F32)
            a = (qw + u_ref[layer].astype(F32)).astype(BF)
            c = (qw + w_ref[layer].astype(F32)).astype(BF)
            rr = rext[pl.ds(pl.multiple_of((seq - 1 - ln) * heads, heads), span)]
            lhs = jnp.concatenate([a, c], axis=1)
            rhs = jnp.concatenate([kbuf[b], rr], axis=1)
            s = lax.dot_general(lhs, rhs, (((1,), (1,)), ((), ())), preferred_element_type=F32)
            score.append(jnp.where(pos <= ln, s * scale, -1e30))
        prob = []
        for g in range(group):
            s = score[g]
            m = jnp.max(s, axis=1, keepdims=True)
            e = jnp.exp(s - m)
            prob.append((e / jnp.sum(e, axis=1, keepdims=True)).astype(BF))
        for g in range(group):
            b = i * group + g
            o = jnp.dot(prob[g], vbuf[b], preferred_element_type=F32)
            ctx_ref[b] = o.astype(BF).astype(F32)
        for c in save(i):
            c.start()

    @pl.loop(0, n_grp)
    def _(i):
        for c in save(i):
            c.wait()


def attend_cache(layer, lengths, q, kn, vn, rel, u, w, k_now, v_now, layers, prev, group=8):
    rows, span, hd = k_now.shape
    heads = q.shape[1]
    seq = span // heads
    any_ = pl.BlockSpec(memory_space=pl.ANY)
    vm = pl.BlockSpec(memory_space=pltpu.VMEM)
    n_grp = rows // group
    k_now, v_now = (pltpu.with_memory_space_constraint(c, pltpu.VMEM) for c in (k_now, v_now))
    ins = [lengths, q, kn, vn, rel, u, w, k_now, v_now]
    specs = [pl.BlockSpec(memory_space=pltpu.SMEM)] + [any_] * 6 + [vm, vm]
    alias = {7: 3, 8: 4}
    if prev is not None:
        ins += prev
        specs += [any_, any_]
        alias.update({9: 1, 10: 2})
    cache = jax.ShapeDtypeStruct((layers, rows, span, hd), BF)
    now = jax.ShapeDtypeStruct(k_now.shape, BF)
    rows_f32 = pltpu.VMEM((rows, heads, hd), F32)
    return pl.pallas_call(
        functools.partial(attn_body, layer, group),
        out_shape=(jax.ShapeDtypeStruct((rows, heads, hd), F32), cache, cache, now, now),
        in_specs=specs, out_specs=(any_, any_, any_, vm, vm), input_output_aliases=alias,
        scratch_shapes=[rows_f32, rows_f32, rows_f32, pltpu.VMEM((seq, heads, hd), BF), pltpu.VMEM(u.shape, BF), pltpu.VMEM(w.shape, BF),
                        rows_f32, pltpu.VMEM((2 * seq * heads, hd), BF), pltpu.SemaphoreType.DMA((6,)), pltpu.SemaphoreType.DMA((3, n_grp))],
        compiler_params=pltpu.CompilerParams(vmem_limit_bytes=VMEM_LIMIT),
        name=f"attend_{layer}")(*ins)[:3]


MESH = pl.DeviceIdType.MESH
EPS = 1e-6
UP_CHUNK = 512
RAW_CHUNK = 512
PIECES = 4
VMEM_LIMIT = 46 << 20


def rows_to_cols(col):
    square = jnp.concatenate([col] * (128 // col.shape[0]), axis=0)
    return jnp.broadcast_to(jnp.sum(square.T, axis=0, keepdims=True), (8, 128))


def cols_to_rows(row, n):
    return jnp.broadcast_to(row[0:1], (128, 128)).T[:n, 0:1]


def stage_body(pre, qkv, layer, names, *refs):
    r = dict(zip(names, refs))
    batch, width = r["hidden"].shape
    ops = ["hidden"] + (["ctx", "g_mlp"] if pre else []) + (["g_attn"] if qkv else [])
    operand = {n: pltpu.make_async_copy(r[n], r["v_" + n], r["op_sem"].at[i]) for i, n in enumerate(ops)}
    for n in ops[::-1]:
        operand[n].start()
    result = {}
    half = width // 2
    rows = batch // 2
    x = lax.axis_index("x")
    y = lax.axis_index("y")
    y_dev = {"y": 1 - y}
    core = x % 2
    pair_dev = {"x": x + 1 - 2 * core}
    far_dev = {"x": x + 1 - 2 * core, "y": 1 - y}
    chip_dev = {"x": (x + 2) % 4}
    qkv_layer = layer + 1 if pre else layer

    def remote(src, dst, sems, idx, dev):
        return pltpu.make_async_remote_copy(src, dst, r[sems].at[0, idx], r[sems].at[1, idx], device_id=dev, device_id_type=MESH)

    def wo_copy(i):
        n = r["wo"].shape[0] // 4
        return pltpu.make_async_copy(r["w_out"].at[layer, pl.ds(i * n, n)], r["wo"].at[pl.ds(i * n, n)], r["wo_sem"].at[i])

    def up_copy(i):
        cols = pl.ds(pl.multiple_of(i * UP_CHUNK, UP_CHUNK), UP_CHUNK)
        return pltpu.make_async_copy(r["w_up"].at[layer, :, cols], r["wup"].at[:, cols], r["wup_sem"].at[i])

    def down_copy(i):
        sl = pl.ds(i * UP_CHUNK, UP_CHUNK)
        return pltpu.make_async_copy(r["w_down"].at[layer, sl], r["wdn"].at[sl], r["wdn_sem"].at[i])

    k_chunks = width // RAW_CHUNK

    def cache_copies(i):
        src, dst = (("k_cache", "k_now"), ("v_cache", "v_now"))[i]
        n = r[dst].shape[0] // 4
        return [pltpu.make_async_copy(r[src].at[qkv_layer, pl.ds(j * n, n)], r[dst].at[pl.ds(j * n, n)], r["cache_sem"].at[i, j]) for j in range(4)]

    def raw_copy(m, i):
        sl = pl.ds(i * RAW_CHUNK, RAW_CHUNK)
        return pltpu.make_async_copy(r[("w_q", "w_k", "w_v")[m]].at[qkv_layer, sl], r["wraw"].at[i], r["wraw_sem"].at[i])

    def start_qkv():
        for i in range(k_chunks):
            raw_copy(0, i).start()

    def flatten(m):
        heads, hd = r["wraw"].shape[2:]

        @pl.loop(0, k_chunks)
        def _(i):
            raw_copy(m, i).wait()

            @pl.loop(0, RAW_CHUNK // 256)
            def _(j):
                off = pl.multiple_of(j * 256, 256)
                by_head = jnp.swapaxes(r["wraw"][i, pl.ds(off, 256)], 0, 1)
                sl = pl.ds(pl.multiple_of(i * RAW_CHUNK + off, 256), 256)
                for hh in range(heads):
                    col = m * heads * hd + hh * hd
                    r["wup"][sl, col:col + hd] = by_head[hh]

            if m < 2:
                raw_copy(m + 1, i).start()

        first = 0 if not pre else 2
        if m == first:
            for c in cache_copies(0):
                c.start()
        if m == min(first + 1, 2):
            for c in cache_copies(1):
                c.start()

    if pre:
        n_up = r["wup"].shape[1] // UP_CHUNK
        for i in range(4):
            wo_copy(i).start()

        @pl.loop(0, n_up)
        def _(i):
            up_copy(i).start()
    else:
        start_qkv()

    barrier = pltpu.get_barrier_semaphore()
    greet = [y_dev, pair_dev, chip_dev, far_dev] if pre else [y_dev]
    for dev in greet:
        pl.semaphore_signal(barrier, inc=1, device_id=dev, device_id_type=MESH)
    pl.semaphore_wait(barrier, len(greet))

    def row_sums(wide):
        sq = wide * wide
        part = sq[:, 0:128]
        for j in range(1, wide.shape[1] // 128):
            part = part + sq[:, j * 128:(j + 1) * 128]
        return part

    def sum_copy(slot, j, dev):
        return pltpu.make_async_remote_copy(r["ss_send"].at[slot], r["ss_recv"].at[slot, j], r["ss_sem"].at[0, slot, j], r["ss_sem"].at[1, slot, j],
                                            device_id=dev, device_id_type=MESH)

    def send_sums(slot, part, devs):
        r["ss_send"][slot] = rows_to_cols(part)
        for j, dev in enumerate(devs):
            sum_copy(slot, j, dev).start()

    def normalize(slot, devs, x_ref, gain_ref, gain_layer):
        for j, dev in enumerate(devs):
            sum_copy(slot, j, dev).wait()
        total = r["ss_send"][slot] + r["ss_recv"][slot, 0]
        if len(devs) > 1:
            total = total + (r["ss_recv"][slot, 1] + r["ss_recv"][slot, 2])
        inv = lax.rsqrt(cols_to_rows(total, batch) / (2 * width) + EPS)
        gain = gain_ref[pl.ds(gain_layer, 1)].astype(F32)
        r["h"][...] = (x_ref[...].astype(F32) * inv * gain).astype(BF)

    cells = [pair_dev, y_dev, far_dev]
    step = half // PIECES

    def piece(side, c):
        return pl.ds(pl.multiple_of(side * half + c * step, step), step)

    def reduce_x(slot, part_of, x_ref, out_ref, sums):
        def copy(kind, c):
            here = pl.ds(c * step, step)
            sems = r[kind + "_sem"]
            if kind == "share":
                src = dst = out_ref.at[:, piece(core, c)]
            else:
                src, dst = r[kind + "_send"].at[slot, :, here], r[kind + "_recv"].at[slot, :, here]
            return pltpu.make_async_remote_copy(src, dst, sems.at[0, slot, c], sems.at[1, slot, c],
                                                device_id=chip_dev if kind == "chip" else pair_dev, device_id_type=MESH)

        r["pair_send"][slot] = part_of(pl.ds(pl.multiple_of((1 - core) * half, half), half)).astype(BF)
        for c in range(PIECES):
            copy("pair", c).start()
        r["part"][...] = part_of(pl.ds(pl.multiple_of(core * half, half), half))
        for c in range(PIECES):
            copy("pair", c).wait()
            here = slice(c * step, (c + 1) * step)
            r["chip_send"][slot, :, here] = (r["part"][:, here] + r["pair_recv"][slot, :, here].astype(F32)).astype(BF)
            copy("chip", c).start()
        part = None
        for c in range(PIECES):
            copy("chip", c).wait()
            here = slice(c * step, (c + 1) * step)
            total = r["chip_send"][slot, :, here].astype(F32) + r["chip_recv"][slot, :, here].astype(F32)
            new = (x_ref[:, piece(core, c)].astype(F32) + total).astype(BF)
            out_ref[:, piece(core, c)] = new
            copy("share", c).start()
            if sums:
                add = row_sums(new.astype(F32))
                part = add if part is None else part + add
        if sums:
            send_sums(slot, part, cells)
        for c in range(PIECES):
            copy("share", c).wait()

    x_now = r["v_hidden"]
    if pre:
        operand["ctx"].wait()
        mine = pl.ds(pl.multiple_of(y * rows, rows), rows)
        heads, hd = r["ctx"].shape[1:]
        for hh in range(heads):
            r["ctx_all"][mine, hh * hd:(hh + 1) * hd] = r["v_ctx"][:, hh, :].astype(BF)
        cp = remote(r["ctx_all"].at[mine], r["ctx_all"].at[mine], "ctx_sem", 0, y_dev)
        cp.start()
        for i in range(4):
            wo_copy(i).wait()
        cp.wait()

        def wo_part(cols):
            return jnp.dot(r["ctx_all"][...], r["wo"][:, cols], preferred_element_type=F32)

        operand["hidden"].wait()
        operand["g_mlp"].wait()
        reduce_x(0, wo_part, r["v_hidden"], r["x_mid"], True)

        @pl.loop(0, n_up)
        def _(i):
            down_copy(i).start()
        if qkv:
            start_qkv()

        normalize(0, cells, r["x_mid"], r["v_g_mlp"], layer)

        def exchange_up(i):
            cols = pl.ds(pl.multiple_of(i * UP_CHUNK, UP_CHUNK), UP_CHUNK)
            return remote(r["up_send"].at[:, cols], r["up_recv"].at[:, cols], "up_sem", i, y_dev)

        @pl.loop(0, n_up)
        def _(i):
            up_copy(i).wait()
            cols = pl.ds(pl.multiple_of(i * UP_CHUNK, UP_CHUNK), UP_CHUNK)
            r["up_send"][:, cols] = jnp.dot(r["h"][...], r["wup"][:, cols], preferred_element_type=F32).astype(BF)
            exchange_up(i).start()

        if qkv:
            for m in range(3):
                flatten(m)

        def activate(i):
            cols = pl.ds(pl.multiple_of(i * UP_CHUNK, UP_CHUNK), UP_CHUNK)
            exchange_up(i).wait()
            m = (r["up_send"][:, cols].astype(F32) + r["up_recv"][:, cols].astype(F32)).astype(BF)
            r["act"][...] = jax.nn.gelu(m.astype(F32), approximate=True).astype(BF)

        r["acc"][...] = jnp.zeros_like(r["acc"])

        @pl.loop(0, n_up - 1)
        def _(i):
            down_copy(i).wait()
            activate(i)
            sl = pl.ds(pl.multiple_of(i * UP_CHUNK, UP_CHUNK), UP_CHUNK)
            r["acc"][...] += jnp.dot(r["act"][...], r["wdn"][sl, :], preferred_element_type=F32)

        down_copy(n_up - 1).wait()
        activate(n_up - 1)

        def down_part(cols):
            last = jnp.dot(r["act"][...], r["wdn"][pl.ds((n_up - 1) * UP_CHUNK, UP_CHUNK), cols], preferred_element_type=F32)
            return r["acc"][:, cols] + last

        reduce_x(1, down_part, r["x_mid"], r["x_end"], qkv)
        result["x_out"] = pltpu.make_async_copy(r["x_end"], r["x_out"], r["out_sem"].at[0])
        result["x_out"].start()
        x_now = r["x_end"]

    if qkv:
        heads, hd = r["wraw"].shape[2:]
        operand["g_attn"].wait()
        if pre:
            normalize(1, cells, x_now, r["v_g_attn"], qkv_layer)
        else:
            operand["hidden"].wait()
            send_sums(1, row_sums(x_now[...].astype(F32)), [y_dev])
            flatten(0)
            normalize(1, [y_dev], x_now, r["v_g_attn"], qkv_layer)
        mine = pl.ds(pl.multiple_of(y * rows, rows), rows)
        theirs = pl.ds(pl.multiple_of((1 - y) * rows, rows), rows)

        def swap(m):
            return remote(r["qkv_send"].at[m], r["qkv_recv"].at[m], "qkv_sem", m, y_dev)

        for m in range(3):
            if not pre and m > 0:
                flatten(m)
            for j in range(heads * hd // 256):
                cols = slice(j * 256, (j + 1) * 256)
                lanes = slice(m * heads * hd + j * 256, m * heads * hd + (j + 1) * 256)
                r["part"][:, cols] = jnp.dot(r["h"][...], r["wup"][:, lanes], preferred_element_type=F32)
            r["qkv_send"][m] = r["part"][theirs, :].astype(BF)
            swap(m).start()
            r["qkv_own"][m] = r["part"][mine, :].astype(BF)

        for m in range(3):
            swap(m).wait()
            full = (r["qkv_own"][m].astype(F32) + r["qkv_recv"][m].astype(F32)).astype(BF).astype(F32)
            name = ("q", "k", "v")[m]
            for hh in range(heads):
                r["v_" + name][:, hh, :] = full[:, hh * hd:(hh + 1) * hd]
            result[name] = pltpu.make_async_copy(r["v_" + name], r[name], r["out_sem"].at[m + 1])
            result[name].start()
        for c in cache_copies(0) + cache_copies(1):
            c.wait()
    for c in result.values():
        c.wait()


def stage(pre, qkv, layer, hidden, ctx, w):
    batch, width = hidden.shape
    heads, hd = w["w_q"].shape[2:]
    rows, half, flat = batch // 2, width // 2, heads * hd
    ff = w["w_up"].shape[2]
    n_up = ff // UP_CHUNK
    vm = pl.BlockSpec(memory_space=pltpu.VMEM)
    any_ = pl.BlockSpec(memory_space=pl.ANY)
    dma = pltpu.SemaphoreType.DMA
    gain = pltpu.VMEM(w["norm_mlp"].shape, BF)
    ins = [("hidden", hidden)]
    outs = []
    scratch = [("ss_send", pltpu.VMEM((2, 8, 128), F32)), ("ss_recv", pltpu.VMEM((2, 3, 8, 128), F32)), ("ss_sem", dma((2, 2, 3))),
               ("h", pltpu.VMEM((batch, width), BF)), ("part", pltpu.VMEM((batch, half), F32)),
               ("v_hidden", pltpu.VMEM((batch, width), BF)), ("op_sem", dma((4,))), ("out_sem", dma((4,))),
               ("wup", pltpu.VMEM((width, ff if pre else 3 * flat), BF))]
    if pre:
        ins += [("ctx", ctx), ("g_mlp", w["norm_mlp"]), ("w_out", w["w_out"]), ("w_up", w["w_up"]), ("w_down", w["w_down"])]
        outs += [("x_out", (batch, width), BF, any_)]
        part = pltpu.VMEM((2, batch, half), BF)
        scratch += [("v_ctx", pltpu.VMEM((rows, heads, hd), F32)), ("v_g_mlp", gain),
                    ("wo", pltpu.VMEM((flat, width), BF)), ("wo_sem", dma((4,))), ("wup_sem", dma((n_up,))),
                    ("wdn", pltpu.VMEM((ff, width), BF)), ("wdn_sem", dma((n_up,))),
                    ("pair_send", part), ("pair_recv", part), ("pair_sem", dma((2, 2, PIECES))),
                    ("chip_send", part), ("chip_recv", part), ("chip_sem", dma((2, 2, PIECES))), ("share_sem", dma((2, 2, PIECES))),
                    ("ctx_all", pltpu.VMEM((batch, flat), BF)), ("ctx_sem", dma((2, 1))),
                    ("x_mid", pltpu.VMEM((batch, width), BF)), ("x_end", pltpu.VMEM((batch, width), BF)),
                    ("up_send", pltpu.VMEM((batch, ff), BF)), ("up_recv", pltpu.VMEM((batch, ff), BF)), ("up_sem", dma((2, n_up))),
                    ("act", pltpu.VMEM((batch, UP_CHUNK), BF)), ("acc", pltpu.VMEM((batch, width), F32))]
    if qkv:
        ins += [("g_attn", w["norm_attn"]), ("w_q", w["w_q"]), ("w_k", w["w_k"]), ("w_v", w["w_v"]), ("k_cache", w["k_cache"]), ("v_cache", w["v_cache"])]
        outs += [(n, (rows, heads, hd), F32, any_) for n in ("q", "k", "v")]
        outs += [(n, w["k_cache"].shape[1:], BF, vm) for n in ("k_now", "v_now")]
        share = pltpu.VMEM((3, rows, flat), BF)
        scratch += [("v_" + n, pltpu.VMEM((rows, heads, hd), F32)) for n in ("q", "k", "v")]
        scratch += [("v_g_attn", gain), ("cache_sem", dma((2, 4))),
                    ("wraw", pltpu.VMEM((width // RAW_CHUNK, RAW_CHUNK, heads, hd), BF)), ("wraw_sem", dma((width // RAW_CHUNK,))),
                    ("qkv_send", share), ("qkv_recv", share), ("qkv_own", share), ("qkv_sem", dma((2, 3)))]
    names = [n for n, *_ in ins] + [n for n, *_ in outs] + [n for n, _ in scratch]
    return pl.pallas_call(
        functools.partial(stage_body, pre, qkv, layer, names),
        out_shape=tuple(pltpu.VMEM(s, d) if n in ("k_now", "v_now") else jax.ShapeDtypeStruct(s, d) for n, s, d, _ in outs),
        in_specs=[any_ for _ in ins],
        out_specs=tuple(o[3] for o in outs),
        scratch_shapes=[s for _, s in scratch],
        compiler_params=pltpu.CompilerParams(collective_id=(1 if pre else 0) + (2 if qkv else 0), has_side_effects=True, vmem_limit_bytes=VMEM_LIMIT),
        name=f"stage_{int(pre)}{int(qkv)}",
    )(*[a for _, a in ins])


def solution(mesh):
    cache_spec = P(None, ("rep", "y"), None, "x", None)
    row_spec = P("rep", "y")
    proj_spec = P(None, "y", "x", None)
    head_spec = P(None, "x", None)
    in_specs = (row_spec, P("rep"), cache_spec, cache_spec, P(None, None, "x", None), P(None, "y"),
                proj_spec, proj_spec, proj_spec, head_spec, head_spec, P(None, "x", None, "y"),
                P(None, "y"), P(None, "y", "x"), P(None, "x", "y"))
    out_specs = (row_spec, cache_spec, cache_spec)

    def local_step(hidden, lengths, k_cache, v_cache, rel_table, norm_attn, w_q, w_k, w_v, bias_content, bias_pos, w_out, norm_mlp, w_up, w_down):
        layers, rows, seq, heads, hd = k_cache.shape
        merged = (layers, rows, seq * heads, hd)
        w = dict(norm_attn=norm_attn, w_q=w_q, w_k=w_k, w_v=w_v, norm_mlp=norm_mlp, w_up=w_up, w_down=w_down,
                 w_out=w_out.reshape(w_out.shape[0], -1, w_out.shape[3]), k_cache=k_cache.reshape(merged), v_cache=v_cache.reshape(merged))
        q, k, v, k_now, v_now = stage(False, True, 0, hidden, None, w)
        prev = None
        for layer in range(layers):
            ctx, *prev = attend_cache(layer, lengths, q, k, v, rel_table, bias_content, bias_pos, k_now, v_now, layers, prev)
            if layer + 1 < layers:
                hidden, q, k, v, k_now, v_now = stage(True, True, layer, hidden, ctx, w)
            else:
                hidden, = stage(True, False, layer, hidden, ctx, w)
        return hidden, prev[0].reshape(k_cache.shape), prev[1].reshape(v_cache.shape)

    return jax.shard_map(local_step, mesh=mesh, in_specs=in_specs, out_specs=out_specs, check_vma=False)
```

time: 152 us -> 121 us (0.80)
  Pallas kernels: 143 us -> 119 us
  local copies, waits for them, and re-layouts: 8.4 us -> 1.62 us
    pallas_call x2, Pallas kernels: 37.4 us -> 19.8 us  [attend_cache(): pl.pallas_call(functools.partial(attn_body, layer, group), out_shape=(jax...]
    unnamed x25 -> x7, local copies, waits for them, and re-layouts: 8.4 us -> 1.62 us
    pallas_call x3, Pallas kernels: 105 us -> 98.8 us  [stage(): pl.pallas_call(functools.partial(stage_body, pre, qkv, layer, names), out...]
where the time goes in v3:
time: 121 us
  Pallas kernels  119 us (98%)
  local copies, waits for them, and re-layouts  1.62 us (1%)
    pallas_call x3, Pallas kernels, stage(): pl.pallas_call(functools.partial(stage_body, pre, qkv, layer, names), out...  98.8 us
    pallas_call x2, Pallas kernels, attend_cache(): pl.pallas_call(functools.partial(attn_body, layer, group), out_shape=(jax...  19.8 us

profile of v3, /device:TPU:0, one launch (start us, length us, event | category | flops | bytes accessed | tf_op | source)
XLA Modules:
  0.0 120.9 jit_solution(13792356885522228766)
XLA Ops:
  0.6 16.7 %stage_01.1 = (f32[32,8,128]{2,1,0:T(8,128)}, f32[32,8,128]{2,1,0:T(8,128)}, f32[32,8,128]{2,1,0:T(8,128)}, bf16[32,1024,128]{2,1,0:T(8,128)(2,1)S(1)}, bf16[32,1024,128]{2,1,0:T(8,128)(2,1)S(1)}) custom-call(bf16[64,2048]{1,0:T(8,128)(2,1)} %refs_0_.3, bf16[2,2048]{1,0:T(2,128)(2,1)} %refs_6_.1, bf16[2,2048,8,128]{3,2,1,0:T(8,128)(2,1)} %refs_7_.1, ...), custom_call_target="tpu_custom_call" | custom-call | tf_op jit(solution)/shard_map/stage_01/pallas_call | solution.py:443
  17.3 9.8 %attend_0.1 = (f32[32,8,128]{2,1,0:T(8,128)}, bf16[2,32,1024,128]{3,2,1,0:T(8,128)(2,1)}, bf16[2,32,1024,128]{3,2,1,0:T(8,128)(2,1)}, bf16[32,1024,128]{2,1,0:T(8,128)(2,1)S(1)}, bf16[32,1024,128]{2,1,0:T(8,128)(2,1)S(1)}) custom-call(s32[64]{0:T(128)} %len_ref.3, ...), custom_call_target="tpu_custom_call", output_to_operand_aliasing={{3}: (7, {}), {4}: (8, {})} | custom-call | tf_op jit(solution)/shard_map/attend_0/pallas_call | solution.py:105
  27.2 46.3 %stage_11.1 = (bf16[64,2048]{1,0:T(8,128)(2,1)}, f32[32,8,128]{2,1,0:T(8,128)}, f32[32,8,128]{2,1,0:T(8,128)}, f32[32,8,128]{2,1,0:T(8,128)}, bf16[32,1024,128]{...) custom-call(bf16[64,2048]{1,0:T(8,128)(2,1)} %refs_0_.3, f32[32,8,128]{2,1,0:T(8,128)} %get-tuple-element.25.refs_1_, ...), custom_call_target="tpu_custom_call" | custom-call | tf_op jit(solution)/shard_map/stage_11/pallas_call | solution.py:443
  73.5 0.0 copy-start
  73.5 0.0 copy-start.2
  73.5 10.0 %attend_1.1 = (f32[32,8,128]{2,1,0:T(8,128)}, bf16[2,32,1024,128]{3,2,1,0:T(8,128)(2,1)}, bf16[2,32,1024,128]{3,2,1,0:T(8,128)(2,1)}, bf16[32,1024,128]{2,1,0:T(8,128)(2,1)S(1)}, bf16[32,1024,128]{2,1,0:T(8,128)(2,1)S(1)}) custom-call(s32[64]{0:T(128)} %len_ref.3, ...), custom_call_target="tpu_custom_call", output_to_operand_aliasing={{3}: (7, {}), {4}: (8, {}), {1}: (9, {}), {2}: (10, {})} | custom-call | tf_op jit(solution)/shard_map/attend_1/pallas_call | solution.py:105
  83.5 0.0 copy-done
  83.5 0.0 copy-done.2
  83.5 0.0 copy-start.1
  83.5 0.9 copy-done.1
  84.4 35.8 %stage_10.1 = bf16[64,2048]{1,0:T(8,128)(2,1)S(1)} custom-call(bf16[64,2048]{1,0:T(8,128)(2,1)S(1)} %copy-done, f32[32,8,128]{2,1,0:T(8,128)S(1)} %copy-done.1, bf16[2,2048]{1,0:T(2,128)(2,1)S(1)} %copy-done.2, bf16[2,1024,2048]{2,1,0:T(8,128)(2,1)} %bitcast.10, bf16[2,2048,4096]{2,1,0:T(8,128)(2,1)} %refs_4_.5, bf16[2,4096,2048]{2,1,0:T(8,128)(2,1)} %refs_5_.3), custom_call_target="tpu_custom_call" | custom-call | tf_op jit(solution)/shard_map/stage_10/pallas_call | solution.py:443
  120.2 0.7 copy.31
Async XLA Ops:
  73.5 10.0 %copy-start = (bf16[64,2048]{1,0:T(8,128)(2,1)S(1)}, bf16[64,2048]{1,0:T(8,128)(2,1)}, u32[]{:S(2)}) copy-start(bf16[64,2048]{1,0:T(8,128)(2,1)} %get-tuple-element.26.refs_0_) | copy-start | bytes 786436
  73.5 10.0 %copy-start.2 = (bf16[2,2048]{1,0:T(2,128)(2,1)S(1)}, bf16[2,2048]{1,0:T(2,128)(2,1)}, u32[]{:S(2)}) copy-start(bf16[2,2048]{1,0:T(2,128)(2,1)} %refs_2_.5) | copy-start | bytes 24580
  83.5 0.9 copy-start.1

commit v4 on v3

--- a/solution.py
+++ b/solution.py
@@ -9,59 +9,44 @@
 BF = jnp.bfloat16
 F32 = jnp.float32
 
-def attn_body(layer, group, len_ref, q_hbm, kn_hbm, vn_hbm, rel_hbm, u_hbm, w_hbm, k_in, v_in, *rest):
-    ctx_hbm, ko, vo, kbuf, vbuf, q_ref, kn_ref, vn_ref, rel_ref, u_ref, w_ref, ctx_ref, rext, osem, wsem = rest[-15:]
+def attn_body(layer, group, len_ref, a_ref, c_ref, kn_ref, vn_ref, rext, k_in, v_in, *rest):
+    ctx_ref, ko, vo, kbuf, vbuf, wsem = rest[-6:]
     rows, span, hd = kbuf.shape
-    heads = q_ref.shape[1]
+    heads = a_ref.shape[1]
     seq = span // heads
     y = lax.axis_index("y")
     n_grp = rows // group
-    small = [(rel_hbm.at[layer], rel_ref), (q_hbm, q_ref), (kn_hbm, kn_ref), (vn_hbm, vn_ref), (u_hbm, u_ref), (w_hbm, w_ref)]
-    small = [pltpu.make_async_copy(src, dst, osem.at[i]) for i, (src, dst) in enumerate(small)]
-    for c in small:
-        c.start()
-
-    def save(i):
-        sl = pl.ds(i * group, group)
-        return (pltpu.make_async_copy(kbuf.at[sl], ko.at[layer, sl], wsem.at[0, i]),
-                pltpu.make_async_copy(vbuf.at[sl], vo.at[layer, sl], wsem.at[1, i]),
-                pltpu.make_async_copy(ctx_ref.at[sl], ctx_hbm.at[sl], wsem.at[2, i]))
-
-    @pl.loop(0, seq, unroll=4)
-    def _(t):
-        rext[pl.ds(pl.multiple_of((seq + t) * heads, heads), heads)] = jnp.zeros((heads, hd), BF)
-
-    small[0].wait()
-
-    @pl.loop(0, seq, unroll=4)
-    def _(t):
-        rext[pl.ds(pl.multiple_of((seq - 1 - t) * heads, heads), heads)] = rel_ref[t]
+
+    @pl.loop(0, rows, unroll=4)
+    def _(b):
+        at = pl.ds(pl.multiple_of(len_ref[y * rows + b] * heads, heads), heads)
+        kbuf[b, at] = kn_ref[b].astype(BF)
+        vbuf[b, at] = vn_ref[b].astype(BF)
 
     col = lax.broadcasted_iota(jnp.int32, (heads, span), 1)
     row = lax.broadcasted_iota(jnp.int32, (heads, span), 0)
     own = (col % heads) == row
     pos = jnp.where(own, col // heads, 1 << 20)
     scale = hd ** -0.5
-    for c in small[1:]:
-        c.wait()
+
+    def save(i):
+        sl = pl.ds(i * group, group)
+        return (pltpu.make_async_copy(kbuf.at[sl], ko.at[layer, sl], wsem.at[0, i]),
+                pltpu.make_async_copy(vbuf.at[sl], vo.at[layer, sl], wsem.at[1, i]))
 
     @pl.loop(0, n_grp)
     def _(i):
-        for g in range(group):
-            b = i * group + g
-            ln = len_ref[y * rows + b]
-            at = pl.ds(pl.multiple_of(ln * heads, heads), heads)
-            kbuf[b, at] = kn_ref[b].astype(BF)
-            vbuf[b, at] = vn_ref[b].astype(BF)
+        for c in save(i):
+            c.start()
+
+    @pl.loop(0, n_grp)
+    def _(i):
         score = []
         for g in range(group):
             b = i * group + g
             ln = len_ref[y * rows + b]
-            qw = q_ref[b].astype(F32)
-            a = (qw + u_ref[layer].astype(F32)).astype(BF)
-            c = (qw + w_ref[layer].astype(F32)).astype(BF)
             rr = rext[pl.ds(pl.multiple_of((seq - 1 - ln) * heads, heads), span)]
-            lhs = jnp.concatenate([a, c], axis=1)
+            lhs = jnp.concatenate([a_ref[b].astype(BF), c_ref[b].astype(BF)], axis=1)
             rhs = jnp.concatenate([kbuf[b], rr], axis=1)
             s = lax.dot_general(lhs, rhs, (((1,), (1,)), ((), ())), preferred_element_type=F32)
             score.append(jnp.where(pos <= ln, s * scale, -1e30))
@@ -75,8 +60,6 @@
             b = i * group + g
             o = jnp.dot(prob[g], vbuf[b], preferred_element_type=F32)
             ctx_ref[b] = o.astype(BF).astype(F32)
-        for c in save(i):
-            c.start()
 
     @pl.loop(0, n_grp)
     def _(i):
@@ -84,40 +67,35 @@
             c.wait()
 
 
-def attend_cache(layer, lengths, q, kn, vn, rel, u, w, k_now, v_now, layers, prev, group=8):
-    rows, span, hd = k_now.shape
-    heads = q.shape[1]
-    seq = span // heads
-    any_ = pl.BlockSpec(memory_space=pl.ANY)
+def attend_cache(layer, lengths, fed, layers, prev, group=8):
+    rows, span, hd = fed[-1].shape
+    heads = fed[0].shape[1]
+    any_ = pl.BlockSpec(memory_space=pltpu.HBM)
     vm = pl.BlockSpec(memory_space=pltpu.VMEM)
     n_grp = rows // group
-    k_now, v_now = (pltpu.with_memory_space_constraint(c, pltpu.VMEM) for c in (k_now, v_now))
-    ins = [lengths, q, kn, vn, rel, u, w, k_now, v_now]
-    specs = [pl.BlockSpec(memory_space=pltpu.SMEM)] + [any_] * 6 + [vm, vm]
-    alias = {7: 3, 8: 4}
+    ins = [lengths] + [pltpu.with_memory_space_constraint(c, pltpu.VMEM) for c in fed]
+    specs = [pl.BlockSpec(memory_space=pltpu.SMEM)] + [vm] * len(fed)
+    alias = {6: 3, 7: 4}
     if prev is not None:
         ins += prev
         specs += [any_, any_]
-        alias.update({9: 1, 10: 2})
+        alias.update({8: 1, 9: 2})
     cache = jax.ShapeDtypeStruct((layers, rows, span, hd), BF)
-    now = jax.ShapeDtypeStruct(k_now.shape, BF)
-    rows_f32 = pltpu.VMEM((rows, heads, hd), F32)
+    now = jax.ShapeDtypeStruct(fed[-1].shape, BF)
     return pl.pallas_call(
         functools.partial(attn_body, layer, group),
-        out_shape=(jax.ShapeDtypeStruct((rows, heads, hd), F32), cache, cache, now, now),
-        in_specs=specs, out_specs=(any_, any_, any_, vm, vm), input_output_aliases=alias,
-        scratch_shapes=[rows_f32, rows_f32, rows_f32, pltpu.VMEM((seq, heads, hd), BF), pltpu.VMEM(u.shape, BF), pltpu.VMEM(w.shape, BF),
-                        rows_f32, pltpu.VMEM((2 * seq * heads, hd), BF), pltpu.SemaphoreType.DMA((6,)), pltpu.SemaphoreType.DMA((3, n_grp))],
-        compiler_params=pltpu.CompilerParams(vmem_limit_bytes=VMEM_LIMIT),
+        out_shape=(pltpu.VMEM((rows, heads, hd), F32), cache, cache, now, now),
+        in_specs=specs, out_specs=(vm, any_, any_, vm, vm), input_output_aliases=alias,
+        scratch_shapes=[pltpu.SemaphoreType.DMA((2, n_grp))],
+        compiler_params=pltpu.CompilerParams(vmem_limit_bytes=24 << 20),
         name=f"attend_{layer}")(*ins)[:3]
 
 
 MESH = pl.DeviceIdType.MESH
 EPS = 1e-6
 UP_CHUNK = 512
-RAW_CHUNK = 512
 PIECES = 4
-VMEM_LIMIT = 46 << 20
+VMEM_LIMIT = 45875200
 
 
 def rows_to_cols(col):
@@ -131,12 +109,11 @@
 
 def stage_body(pre, qkv, layer, names, *refs):
     r = dict(zip(names, refs))
-    batch, width = r["hidden"].shape
-    ops = ["hidden"] + (["ctx", "g_mlp"] if pre else []) + (["g_attn"] if qkv else [])
-    operand = {n: pltpu.make_async_copy(r[n], r["v_" + n], r["op_sem"].at[i]) for i, n in enumerate(ops)}
-    for n in ops[::-1]:
+    batch, width = r["h"].shape
+    ops = [n[2:] for n in names if n.startswith("v_") and n[2:] in names]
+    operand = {n: pltpu.make_async_copy(r[n] if n != "rel" else r[n].at[layer + int(pre)], r["v_" + n], r["op_sem"].at[i]) for i, n in enumerate(ops)}
+    for n in ops:
         operand[n].start()
-    result = {}
     half = width // 2
     rows = batch // 2
     x = lax.axis_index("x")
@@ -163,39 +140,42 @@
         sl = pl.ds(i * UP_CHUNK, UP_CHUNK)
         return pltpu.make_async_copy(r["w_down"].at[layer, sl], r["wdn"].at[sl], r["wdn_sem"].at[i])
 
-    k_chunks = width // RAW_CHUNK
+    slots, raw_rows = r["wraw"].shape[:2] if qkv else (1, width)
+    turns = width // (slots * raw_rows)
 
     def cache_copies(i):
         src, dst = (("k_cache", "k_now"), ("v_cache", "v_now"))[i]
         n = r[dst].shape[0] // 4
         return [pltpu.make_async_copy(r[src].at[qkv_layer, pl.ds(j * n, n)], r[dst].at[pl.ds(j * n, n)], r["cache_sem"].at[i, j]) for j in range(4)]
 
-    def raw_copy(m, i):
-        sl = pl.ds(i * RAW_CHUNK, RAW_CHUNK)
-        return pltpu.make_async_copy(r[("w_q", "w_k", "w_v")[m]].at[qkv_layer, sl], r["wraw"].at[i], r["wraw_sem"].at[i])
+    def raw_copy(m, turn, j):
+        sl = pl.ds((turn * slots + j) * raw_rows, raw_rows)
+        return pltpu.make_async_copy(r[("w_q", "w_k", "w_v")[m]].at[qkv_layer, sl], r["wraw"].at[j], r["wraw_sem"].at[j])
 
     def start_qkv():
-        for i in range(k_chunks):
-            raw_copy(0, i).start()
+        for j in range(slots):
+            raw_copy(0, 0, j).start()
 
     def flatten(m):
         heads, hd = r["wraw"].shape[2:]
-
-        @pl.loop(0, k_chunks)
-        def _(i):
-            raw_copy(m, i).wait()
-
-            @pl.loop(0, RAW_CHUNK // 256)
+        for turn in range(turns):
+            after = (m, turn + 1) if turn + 1 < turns else (m + 1, 0)
+
+            @pl.loop(0, slots)
             def _(j):
-                off = pl.multiple_of(j * 256, 256)
-                by_head = jnp.swapaxes(r["wraw"][i, pl.ds(off, 256)], 0, 1)
-                sl = pl.ds(pl.multiple_of(i * RAW_CHUNK + off, 256), 256)
-                for hh in range(heads):
-                    col = m * heads * hd + hh * hd
-                    r["wup"][sl, col:col + hd] = by_head[hh]
-
-            if m < 2:
-                raw_copy(m + 1, i).start()
+                raw_copy(m, turn, j).wait()
+
+                @pl.loop(0, raw_rows // 256)
+                def _(b):
+                    off = pl.multiple_of(b * 256, 256)
+                    by_head = jnp.swapaxes(r["wraw"][j, pl.ds(off, 256)], 0, 1)
+                    sl = pl.ds(pl.multiple_of((turn * slots + j) * raw_rows + off, 256), 256)
+                    for hh in range(heads):
+                        col = m * heads * hd + hh * hd
+                        r["wup"][sl, col:col + hd] = by_head[hh]
+
+                if after[0] < 3:
+                    raw_copy(*after, j).start()
 
         first = 0 if not pre else 2
         if m == first:
@@ -204,6 +184,15 @@
         if m == min(first + 1, 2):
             for c in cache_copies(1):
                 c.start()
+
+    def reverse_rel():
+        operand["rel"].wait()
+        seq, heads, hd = r["v_rel"].shape
+
+        @pl.loop(0, seq, unroll=4)
+        def _(t):
+            r["rext"][pl.ds(pl.multiple_of((seq - 1 - t) * heads, heads), heads)] = r["v_rel"][t]
+            r["rext"][pl.ds(pl.multiple_of((seq + t) * heads, heads), heads)] = jnp.zeros((heads, hd), BF)
 
     if pre:
         n_up = r["wup"].shape[1] // UP_CHUNK
@@ -290,13 +279,12 @@
         for c in range(PIECES):
             copy("share", c).wait()
 
-    x_now = r["v_hidden"]
+    x_now = r["v_hidden"] if "hidden" in ops else r["hidden"]
     if pre:
-        operand["ctx"].wait()
         mine = pl.ds(pl.multiple_of(y * rows, rows), rows)
         heads, hd = r["ctx"].shape[1:]
         for hh in range(heads):
-            r["ctx_all"][mine, hh * hd:(hh + 1) * hd] = r["v_ctx"][:, hh, :].astype(BF)
+            r["ctx_all"][mine, hh * hd:(hh + 1) * hd] = r["ctx"][:, hh, :].astype(BF)
         cp = remote(r["ctx_all"].at[mine], r["ctx_all"].at[mine], "ctx_sem", 0, y_dev)
         cp.start()
         for i in range(4):
@@ -306,9 +294,10 @@
         def wo_part(cols):
             return jnp.dot(r["ctx_all"][...], r["wo"][:, cols], preferred_element_type=F32)
 
-        operand["hidden"].wait()
+        if "hidden" in ops:
+            operand["hidden"].wait()
         operand["g_mlp"].wait()
-        reduce_x(0, wo_part, r["v_hidden"], r["x_mid"], True)
+        reduce_x(0, wo_part, x_now, r["x_mid"], True)
 
         @pl.loop(0, n_up)
         def _(i):
@@ -332,6 +321,7 @@
         if qkv:
             for m in range(3):
                 flatten(m)
+            reverse_rel()
 
         def activate(i):
             cols = pl.ds(pl.multiple_of(i * UP_CHUNK, UP_CHUNK), UP_CHUNK)
@@ -356,8 +346,7 @@
             return r["acc"][:, cols] + last
 
         reduce_x(1, down_part, r["x_mid"], r["x_end"], qkv)
-        result["x_out"] = pltpu.make_async_copy(r["x_end"], r["x_out"], r["out_sem"].at[0])
-        result["x_out"].start()
+        r["x_out"][...] = r["x_end"][...]
         x_now = r["x_end"]
 
     if qkv:
@@ -387,18 +376,22 @@
             swap(m).start()
             r["qkv_own"][m] = r["part"][mine, :].astype(BF)
 
+        if not pre:
+            reverse_rel()
+        operand["bias_u"].wait()
+        operand["bias_w"].wait()
         for m in range(3):
             swap(m).wait()
             full = (r["qkv_own"][m].astype(F32) + r["qkv_recv"][m].astype(F32)).astype(BF).astype(F32)
-            name = ("q", "k", "v")[m]
             for hh in range(heads):
-                r["v_" + name][:, hh, :] = full[:, hh * hd:(hh + 1) * hd]
-            result[name] = pltpu.make_async_copy(r["v_" + name], r[name], r["out_sem"].at[m + 1])
-            result[name].start()
+                head = full[:, hh * hd:(hh + 1) * hd]
+                if m:
+                    r[("k", "v")[m - 1]][:, hh, :] = head
+                else:
+                    r["a"][:, hh, :] = (head + r["v_bias_u"][qkv_layer, hh:hh + 1].astype(F32)).astype(BF).astype(F32)
+                    r["c"][:, hh, :] = (head + r["v_bias_w"][qkv_layer, hh:hh + 1].astype(F32)).astype(BF).astype(F32)
         for c in cache_copies(0) + cache_copies(1):
             c.wait()
-    for c in result.values():
-        c.wait()
 
 
 def stage(pre, qkv, layer, hidden, ctx, w):
@@ -408,20 +401,23 @@
     ff = w["w_up"].shape[2]
     n_up = ff // UP_CHUNK
     vm = pl.BlockSpec(memory_space=pltpu.VMEM)
-    any_ = pl.BlockSpec(memory_space=pl.ANY)
+    any_ = pl.BlockSpec(memory_space=pltpu.HBM)
     dma = pltpu.SemaphoreType.DMA
     gain = pltpu.VMEM(w["norm_mlp"].shape, BF)
     ins = [("hidden", hidden)]
+    placed = {"ctx"} if layer == 0 else {"ctx", "hidden"}
     outs = []
     scratch = [("ss_send", pltpu.VMEM((2, 8, 128), F32)), ("ss_recv", pltpu.VMEM((2, 3, 8, 128), F32)), ("ss_sem", dma((2, 2, 3))),
                ("h", pltpu.VMEM((batch, width), BF)), ("part", pltpu.VMEM((batch, half), F32)),
-               ("v_hidden", pltpu.VMEM((batch, width), BF)), ("op_sem", dma((4,))), ("out_sem", dma((4,))),
+               ("op_sem", dma((6,))),
                ("wup", pltpu.VMEM((width, ff if pre else 3 * flat), BF))]
+    if "hidden" not in placed:
+        scratch += [("v_hidden", pltpu.VMEM((batch, width), BF))]
     if pre:
         ins += [("ctx", ctx), ("g_mlp", w["norm_mlp"]), ("w_out", w["w_out"]), ("w_up", w["w_up"]), ("w_down", w["w_down"])]
-        outs += [("x_out", (batch, width), BF, any_)]
+        outs += [("x_out", (batch, width), BF)]
         part = pltpu.VMEM((2, batch, half), BF)
-        scratch += [("v_ctx", pltpu.VMEM((rows, heads, hd), F32)), ("v_g_mlp", gain),
+        scratch += [("v_g_mlp", gain),
                     ("wo", pltpu.VMEM((flat, width), BF)), ("wo_sem", dma((4,))), ("wup_sem", dma((n_up,))),
                     ("wdn", pltpu.VMEM((ff, width), BF)), ("wdn_sem", dma((n_up,))),
                     ("pair_send", part), ("pair_recv", part), ("pair_sem", dma((2, 2, PIECES))),
@@ -432,23 +428,28 @@
                     ("act", pltpu.VMEM((batch, UP_CHUNK), BF)), ("acc", pltpu.VMEM((batch, width), F32))]
     if qkv:
         ins += [("g_attn", w["norm_attn"]), ("w_q", w["w_q"]), ("w_k", w["w_k"]), ("w_v", w["w_v"]), ("k_cache", w["k_cache"]), ("v_cache", w["v_cache"])]
-        outs += [(n, (rows, heads, hd), F32, any_) for n in ("q", "k", "v")]
-        outs += [(n, w["k_cache"].shape[1:], BF, vm) for n in ("k_now", "v_now")]
+        ins += [("rel", w["rel"]), ("bias_u", w["bias_u"]), ("bias_w", w["bias_w"])]
+        seq = w["rel"].shape[1]
+        outs += [(n, (rows, heads, hd), F32) for n in ("a", "c", "k", "v")]
+        outs += [("rext", (2 * seq * heads, hd), BF)]
+        outs += [(n, w["k_cache"].shape[1:], BF) for n in ("k_now", "v_now")]
         share = pltpu.VMEM((3, rows, flat), BF)
-        scratch += [("v_" + n, pltpu.VMEM((rows, heads, hd), F32)) for n in ("q", "k", "v")]
+        scratch += [("v_" + n, pltpu.VMEM(w[n].shape, BF)) for n in ("bias_u", "bias_w")]
+        scratch += [("v_rel", pltpu.VMEM((seq, heads, hd), BF))]
         scratch += [("v_g_attn", gain), ("cache_sem", dma((2, 4))),
-                    ("wraw", pltpu.VMEM((width // RAW_CHUNK, RAW_CHUNK, heads, hd), BF)), ("wraw_sem", dma((width // RAW_CHUNK,))),
+                    ("wraw", pltpu.VMEM((4, 256 if pre else 512, heads, hd), BF)), ("wraw_sem", dma((4,))),
                     ("qkv_send", share), ("qkv_recv", share), ("qkv_own", share), ("qkv_sem", dma((2, 3)))]
     names = [n for n, *_ in ins] + [n for n, *_ in outs] + [n for n, _ in scratch]
+    args = [pltpu.with_memory_space_constraint(a, pltpu.VMEM if n in placed else pltpu.HBM) for n, a in ins]
     return pl.pallas_call(
         functools.partial(stage_body, pre, qkv, layer, names),
-        out_shape=tuple(pltpu.VMEM(s, d) if n in ("k_now", "v_now") else jax.ShapeDtypeStruct(s, d) for n, s, d, _ in outs),
-        in_specs=[any_ for _ in ins],
-        out_specs=tuple(o[3] for o in outs),
+        out_shape=tuple(pltpu.VMEM(s, d) if qkv else jax.ShapeDtypeStruct(s, d) for _, s, d in outs),
+        in_specs=[vm if n in placed else any_ for n, _ in ins],
+        out_specs=tuple(vm for _ in outs),
         scratch_shapes=[s for _, s in scratch],
         compiler_params=pltpu.CompilerParams(collective_id=(1 if pre else 0) + (2 if qkv else 0), has_side_effects=True, vmem_limit_bytes=VMEM_LIMIT),
         name=f"stage_{int(pre)}{int(qkv)}",
-    )(*[a for _, a in ins])
+    )(*args)
 
 
 def solution(mesh):
@@ -465,13 +466,14 @@
         layers, rows, seq, heads, hd = k_cache.shape
         merged = (layers, rows, seq * heads, hd)
         w = dict(norm_attn=norm_attn, w_q=w_q, w_k=w_k, w_v=w_v, norm_mlp=norm_mlp, w_up=w_up, w_down=w_down,
-                 w_out=w_out.reshape(w_out.shape[0], -1, w_out.shape[3]), k_cache=k_cache.reshape(merged), v_cache=v_cache.reshape(merged))
-        q, k, v, k_now, v_now = stage(False, True, 0, hidden, None, w)
+                 w_out=w_out.reshape(w_out.shape[0], -1, w_out.shape[3]), k_cache=k_cache.reshape(merged), v_cache=v_cache.reshape(merged),
+                 rel=rel_table, bias_u=bias_content, bias_w=bias_pos)
+        fed = stage(False, True, 0, hidden, None, w)
         prev = None
         for layer in range(layers):
-            ctx, *prev = attend_cache(layer, lengths, q, k, v, rel_table, bias_content, bias_pos, k_now, v_now, layers, prev)
+            ctx, *prev = attend_cache(layer, lengths, fed, layers, prev)
             if layer + 1 < layers:
-                hidden, q, k, v, k_now, v_now = stage(True, True, layer, hidden, ctx, w)
+                hidden, *fed = stage(True, True, layer, hidden, ctx, w)
             else:
                 hidden, = stage(True, False, layer, hidden, ctx, w)
         return hidden, prev[0].reshape(k_cache.shape), prev[1].reshape(v_cache.shape)

time: 121 us -> 114 us (0.942)
  Pallas kernels: 119 us -> 112 us
    pallas_call x2, Pallas kernels: 19.8 us -> 13.9 us  [attend_cache(): pl.pallas_call(functools.partial(attn_body, layer, group), out_shape=(plt...]
where the time goes in v4:
time: 114 us; the launch traced here: 113 us
  Pallas kernels  112 us (98%)
    pallas_call x3, Pallas kernels, stage(): pl.pallas_call(functools.partial(stage_body, pre, qkv, layer, names), out...  98.2 us
    pallas_call x2, Pallas kernels, attend_cache(): pl.pallas_call(functools.partial(attn_body, layer, group), out_shape=(plt...  13.9 us

profile of v4, /device:TPU:0, one launch (start us, length us, event | category | flops | bytes accessed | tf_op | source)
XLA Modules:
  0.0 113.4 jit_solution(10535545329655961627)
XLA Ops:
  0.6 0.0 copy-start
  0.6 16.0 %stage_01.1 = (f32[32,8,128]{2,1,0:T(8,128)S(1)}, f32[32,8,128]{2,1,0:T(8,128)S(1)}, f32[32,8,128]{2,1,0:T(8,128)S(1)}, f32[32,8,128]{2,1,0:T(8,128)S(1)}, bf16[...) custom-call(bf16[64,2048]{1,0:T(8,128)(2,1)} %refs_0_.3, ...), custom_call_target="tpu_custom_call" | custom-call | tf_op jit(solution)/shard_map/stage_01/pallas_call | solution.py:444
  16.6 0.0 copy-done
  16.6 6.9 %attend_0.1 = (f32[32,8,128]{2,1,0:T(8,128)S(1)}, bf16[2,32,1024,128]{3,2,1,0:T(8,128)(2,1)}, bf16[2,32,1024,128]{3,2,1,0:T(8,128)(2,1)}, bf16[32,1024,128]{2,1,0:T(8,128)(2,1)S(1)}, bf16[32,1024,128]{2,1,0:T(8,128)(2,1)S(1)}) custom-call(s32[64]{0:T(128)S(1)} %copy-done, ...), custom_call_target="tpu_custom_call", output_to_operand_aliasing={{3}: (6, {}), {4}: (7, {})} | custom-call | tf_op jit(solution)/shard_map/attend_0/pallas_call | solution.py:85
  23.6 46.6 %stage_11.1 = (bf16[64,2048]{1,0:T(8,128)(2,1)S(1)}, f32[32,8,128]{2,1,0:T(8,128)S(1)}, f32[32,8,128]{2,1,0:T(8,128)S(1)}, f32[32,8,128]{2,1,0:T(8,128)S(1)}, f3...) custom-call(bf16[64,2048]{1,0:T(8,128)(2,1)} %refs_0_.3, ...), custom_call_target="tpu_custom_call" | custom-call | tf_op jit(solution)/shard_map/stage_11/pallas_call | solution.py:444
  70.2 6.9 %attend_1.1 = (f32[32,8,128]{2,1,0:T(8,128)S(1)}, bf16[2,32,1024,128]{3,2,1,0:T(8,128)(2,1)}, bf16[2,32,1024,128]{3,2,1,0:T(8,128)(2,1)}, bf16[32,1024,128]{2,1,0:T(8,128)(2,1)S(1)}, bf16[32,1024,128]{2,1,0:T(8,128)(2,1)S(1)}) custom-call(s32[64]{0:T(128)S(1)} %copy-done, ...), custom_call_target="tpu_custom_call", output_to_operand_aliasing={{3}: (6, {}), {4}: (7, {}), {1}: (8, {}), {2}: (9, {})} | custom-call | tf_op jit(solution)/shard_map/attend_1/pallas_call | solution.py:85
  77.1 35.6 %stage_10.1 = bf16[64,2048]{1,0:T(8,128)(2,1)S(1)} custom-call(bf16[64,2048]{1,0:T(8,128)(2,1)S(1)} %get-tuple-element.32.refs_0_, f32[32,8,128]{2,1,0:T(8,128)S(1)} %get-tuple-element.42.refs_1_, bf16[2,2048]{1,0:T(2,128)(2,1)} %refs_2_.5, bf16[2,1024,2048]{2,1,0:T(8,128)(2,1)} %bitcast.10, bf16[2,2048,4096]{2,1,0:T(8,128)(2,1)} %refs_4_.5, ...), custom_call_target="tpu_custom_call" | custom-call | tf_op jit(solution)/shard_map/stage_10/pallas_call | solution.py:444
  112.7 0.7 copy.31
Async XLA Ops:
  0.6 16.0 %copy-start = (s32[64]{0:T(128)S(1)}, s32[64]{0:T(128)}, u32[]{:S(2)}) copy-start(s32[64]{0:T(128)} %len_ref.3) | copy-start | bytes 772

commit v5 on v4

--- a/solution.py
+++ b/solution.py
@@ -94,7 +94,6 @@
 MESH = pl.DeviceIdType.MESH
 EPS = 1e-6
 UP_CHUNK = 512
-PIECES = 4
 VMEM_LIMIT = 45875200
 
 
@@ -121,7 +120,9 @@
     y_dev = {"y": 1 - y}
     core = x % 2
     pair_dev = {"x": x + 1 - 2 * core}
-    far_dev = {"x": x + 1 - 2 * core, "y": 1 - y}
+    mine = pl.ds(pl.multiple_of(y * rows, rows), rows)
+    theirs = pl.ds(pl.multiple_of((1 - y) * rows, rows), rows)
+    everyone = pl.ds(0, batch)
     chip_dev = {"x": (x + 2) % 4}
     qkv_layer = layer + 1 if pre else layer
 
@@ -177,12 +178,8 @@
                 if after[0] < 3:
                     raw_copy(*after, j).start()
 
-        first = 0 if not pre else 2
-        if m == first:
-            for c in cache_copies(0):
-                c.start()
-        if m == min(first + 1, 2):
-            for c in cache_copies(1):
+        if m < 2:
+            for c in cache_copies(m):
                 c.start()
 
     def reverse_rel():
@@ -206,7 +203,7 @@
         start_qkv()
 
     barrier = pltpu.get_barrier_semaphore()
-    greet = [y_dev, pair_dev, chip_dev, far_dev] if pre else [y_dev]
+    greet = [y_dev, pair_dev, chip_dev] if pre else [y_dev]
     for dev in greet:
         pl.semaphore_signal(barrier, inc=1, device_id=dev, device_id_type=MESH)
     pl.semaphore_wait(barrier, len(greet))
@@ -218,116 +215,134 @@
             part = part + sq[:, j * 128:(j + 1) * 128]
         return part
 
-    def sum_copy(slot, j, dev):
-        return pltpu.make_async_remote_copy(r["ss_send"].at[slot], r["ss_recv"].at[slot, j], r["ss_sem"].at[0, slot, j], r["ss_sem"].at[1, slot, j],
-                                            device_id=dev, device_id_type=MESH)
-
-    def send_sums(slot, part, devs):
-        r["ss_send"][slot] = rows_to_cols(part)
-        for j, dev in enumerate(devs):
-            sum_copy(slot, j, dev).start()
-
-    def normalize(slot, devs, x_ref, gain_ref, gain_layer):
-        for j, dev in enumerate(devs):
-            sum_copy(slot, j, dev).wait()
-        total = r["ss_send"][slot] + r["ss_recv"][slot, 0]
-        if len(devs) > 1:
-            total = total + (r["ss_recv"][slot, 1] + r["ss_recv"][slot, 2])
-        inv = lax.rsqrt(cols_to_rows(total, batch) / (2 * width) + EPS)
+    def sum_copy(slot):
+        return remote(r["ss_send"].at[slot], r["ss_recv"].at[slot], "ss_sem", slot, y_dev)
+
+    def inv_rms(sums, n):
+        return lax.rsqrt(cols_to_rows(sums, n) / (2 * width) + EPS)
+
+    def normalize(slot, x_ref, at, n, gain_ref, gain_layer):
+        wide = x_ref[at].astype(F32)
+        r["ss_send"][slot] = rows_to_cols(row_sums(wide))
+        sum_copy(slot).start()
         gain = gain_ref[pl.ds(gain_layer, 1)].astype(F32)
-        r["h"][...] = (x_ref[...].astype(F32) * inv * gain).astype(BF)
-
-    cells = [pair_dev, y_dev, far_dev]
-    step = half // PIECES
-
-    def piece(side, c):
-        return pl.ds(pl.multiple_of(side * half + c * step, step), step)
-
-    def reduce_x(slot, part_of, x_ref, out_ref, sums):
-        def copy(kind, c):
-            here = pl.ds(c * step, step)
+        r["h"][at] = (x_ref[at].astype(F32) * inv_rms(r["ss_send"][slot], n) * gain).astype(BF)
+
+    def factors(own_sums, peer_sums, n):
+        whole = inv_rms(own_sums + peer_sums, n)
+        return whole / inv_rms(own_sums, n), whole / inv_rms(peer_sums, n)
+
+    def half_of(side):
+        return pl.ds(pl.multiple_of(side * half, half), half)
+
+    def reducer(slot, bank, at, pieces, part_of, x_ref, out_ref):
+        step = half // pieces
+
+        def copy(kind, c=0):
+            here = pl.ds(c * step, step) if kind == "chip" else pl.ds(0, half)
+            if kind == "share":
+                src = dst = out_ref.at[at, pl.ds(pl.multiple_of(core * half + c * step, step), step)]
+            else:
+                src, dst = r[kind + "_send"].at[bank, at, here], r[kind + "_recv"].at[bank, at, here]
             sems = r[kind + "_sem"]
-            if kind == "share":
-                src = dst = out_ref.at[:, piece(core, c)]
-            else:
-                src, dst = r[kind + "_send"].at[slot, :, here], r[kind + "_recv"].at[slot, :, here]
             return pltpu.make_async_remote_copy(src, dst, sems.at[0, slot, c], sems.at[1, slot, c],
                                                 device_id=chip_dev if kind == "chip" else pair_dev, device_id_type=MESH)
 
-        r["pair_send"][slot] = part_of(pl.ds(pl.multiple_of((1 - core) * half, half), half)).astype(BF)
-        for c in range(PIECES):
-            copy("pair", c).start()
-        r["part"][...] = part_of(pl.ds(pl.multiple_of(core * half, half), half))
-        for c in range(PIECES):
-            copy("pair", c).wait()
-            here = slice(c * step, (c + 1) * step)
-            r["chip_send"][slot, :, here] = (r["part"][:, here] + r["pair_recv"][slot, :, here].astype(F32)).astype(BF)
-            copy("chip", c).start()
-        part = None
-        for c in range(PIECES):
-            copy("chip", c).wait()
-            here = slice(c * step, (c + 1) * step)
-            total = r["chip_send"][slot, :, here].astype(F32) + r["chip_recv"][slot, :, here].astype(F32)
-            new = (x_ref[:, piece(core, c)].astype(F32) + total).astype(BF)
-            out_ref[:, piece(core, c)] = new
-            copy("share", c).start()
-            if sums:
-                add = row_sums(new.astype(F32))
-                part = add if part is None else part + add
-        if sums:
-            send_sums(slot, part, cells)
-        for c in range(PIECES):
-            copy("share", c).wait()
+        def begin():
+            r["pair_send"][bank, at] = part_of(half_of(1 - core)).astype(BF)
+            copy("pair").start()
+            r["part"][at] = part_of(half_of(core))
+
+        def cross():
+            copy("pair").wait()
+            for c in range(pieces):
+                here = slice(c * step, (c + 1) * step)
+                r["chip_send"][bank, at, here] = (r["part"][at, here] + r["pair_recv"][bank, at, here].astype(F32)).astype(BF)
+                copy("chip", c).start()
+
+        def land():
+            for c in range(pieces):
+                copy("chip", c).wait()
+                here = slice(c * step, (c + 1) * step)
+                cols = pl.ds(pl.multiple_of(core * half + c * step, step), step)
+                total = r["chip_send"][bank, at, here].astype(F32) + r["chip_recv"][bank, at, here].astype(F32)
+                out_ref[at, cols] = (x_ref[at, cols].astype(F32) + total).astype(BF)
+                copy("share", c).start()
+
+        def finish():
+            for c in range(pieces):
+                copy("share", c).wait()
+
+        return begin, cross, land, finish
 
     x_now = r["v_hidden"] if "hidden" in ops else r["hidden"]
     if pre:
-        mine = pl.ds(pl.multiple_of(y * rows, rows), rows)
         heads, hd = r["ctx"].shape[1:]
         for hh in range(heads):
             r["ctx_all"][mine, hh * hd:(hh + 1) * hd] = r["ctx"][:, hh, :].astype(BF)
-        cp = remote(r["ctx_all"].at[mine], r["ctx_all"].at[mine], "ctx_sem", 0, y_dev)
-        cp.start()
+        ctx_copy = remote(r["ctx_all"].at[mine], r["ctx_all"].at[mine], "ctx_sem", 0, y_dev)
+        ctx_copy.start()
+
+        def wo_part(at):
+            return lambda cols: jnp.dot(r["ctx_all"][at], r["wo"][:, cols], preferred_element_type=F32)
+
+        near = reducer(0, 0, mine, 2, wo_part(mine), x_now, r["x_mid"])
+        far = reducer(1, 0, theirs, 2, wo_part(theirs), x_now, r["x_mid"])
         for i in range(4):
             wo_copy(i).wait()
-        cp.wait()
-
-        def wo_part(cols):
-            return jnp.dot(r["ctx_all"][...], r["wo"][:, cols], preferred_element_type=F32)
-
-        if "hidden" in ops:
-            operand["hidden"].wait()
-        operand["g_mlp"].wait()
-        reduce_x(0, wo_part, x_now, r["x_mid"], True)
+        near[0]()
+        near[1]()
 
         @pl.loop(0, n_up)
         def _(i):
             down_copy(i).start()
         if qkv:
             start_qkv()
-
-        normalize(0, cells, r["x_mid"], r["v_g_mlp"], layer)
-
-        def exchange_up(i):
+        ctx_copy.wait()
+        far[0]()
+        far[1]()
+        if "hidden" in ops:
+            operand["hidden"].wait()
+        operand["g_mlp"].wait()
+
+        def exchange_up(g, at, i):
             cols = pl.ds(pl.multiple_of(i * UP_CHUNK, UP_CHUNK), UP_CHUNK)
-            return remote(r["up_send"].at[:, cols], r["up_recv"].at[:, cols], "up_sem", i, y_dev)
-
-        @pl.loop(0, n_up)
-        def _(i):
-            up_copy(i).wait()
-            cols = pl.ds(pl.multiple_of(i * UP_CHUNK, UP_CHUNK), UP_CHUNK)
-            r["up_send"][:, cols] = jnp.dot(r["h"][...], r["wup"][:, cols], preferred_element_type=F32).astype(BF)
-            exchange_up(i).start()
+            return pltpu.make_async_remote_copy(r["up_send"].at[at, cols], r["up_recv"].at[at, cols], r["up_sem"].at[0, g, i], r["up_sem"].at[1, g, i],
+                                                device_id=y_dev, device_id_type=MESH)
+
+        def send_up(g, at):
+            normalize(g, r["x_mid"], at, rows, r["v_g_mlp"], layer)
+
+            @pl.loop(0, n_up)
+            def _(i):
+                if g == 0:
+                    up_copy(i).wait()
+                cols = pl.ds(pl.multiple_of(i * UP_CHUNK, UP_CHUNK), UP_CHUNK)
+                r["up_send"][at, cols] = jnp.dot(r["h"][at], r["wup"][:, cols], preferred_element_type=F32).astype(BF)
+                exchange_up(g, at, i).start()
+
+        near[2]()
+        near[3]()
+        send_up(0, mine)
+        far[2]()
+        far[3]()
+        send_up(1, theirs)
 
         if qkv:
-            for m in range(3):
-                flatten(m)
-            reverse_rel()
+            flatten(0)
+
+        for g in range(2):
+            sum_copy(g).wait()
+        for g, at in enumerate((mine, theirs)):
+            for j, f in enumerate(factors(r["ss_send"][g], r["ss_recv"][1 - g], rows)):
+                r["fac"][j, at] = jnp.broadcast_to(f, (rows, 128))
 
         def activate(i):
             cols = pl.ds(pl.multiple_of(i * UP_CHUNK, UP_CHUNK), UP_CHUNK)
-            exchange_up(i).wait()
-            m = (r["up_send"][:, cols].astype(F32) + r["up_recv"][:, cols].astype(F32)).astype(BF)
-            r["act"][...] = jax.nn.gelu(m.astype(F32), approximate=True).astype(BF)
+            exchange_up(0, mine, i).wait()
+            exchange_up(1, theirs, i).wait()
+            m = r["up_send"][:, cols].astype(F32) * r["fac"][0][:, 0:1] + r["up_recv"][:, cols].astype(F32) * r["fac"][1][:, 0:1]
+            r["act"][...] = jax.nn.gelu(m.astype(BF).astype(F32), approximate=True).astype(BF)
 
         r["acc"][...] = jnp.zeros_like(r["acc"])
 
@@ -345,28 +360,30 @@
             last = jnp.dot(r["act"][...], r["wdn"][pl.ds((n_up - 1) * UP_CHUNK, UP_CHUNK), cols], preferred_element_type=F32)
             return r["acc"][:, cols] + last
 
-        reduce_x(1, down_part, r["x_mid"], r["x_end"], qkv)
+        begin, cross, land, finish = reducer(2, 1, everyone, 4, down_part, r["x_mid"], r["x_end"])
+        begin()
+        cross()
+        if qkv:
+            flatten(1)
+            flatten(2)
+            reverse_rel()
+        land()
+        finish()
         r["x_out"][...] = r["x_end"][...]
         x_now = r["x_end"]
 
     if qkv:
         heads, hd = r["wraw"].shape[2:]
         operand["g_attn"].wait()
-        if pre:
-            normalize(1, cells, x_now, r["v_g_attn"], qkv_layer)
-        else:
+        if not pre:
             operand["hidden"].wait()
-            send_sums(1, row_sums(x_now[...].astype(F32)), [y_dev])
-            flatten(0)
-            normalize(1, [y_dev], x_now, r["v_g_attn"], qkv_layer)
-        mine = pl.ds(pl.multiple_of(y * rows, rows), rows)
-        theirs = pl.ds(pl.multiple_of((1 - y) * rows, rows), rows)
+        normalize(2, x_now, everyone, batch, r["v_g_attn"], qkv_layer)
 
         def swap(m):
             return remote(r["qkv_send"].at[m], r["qkv_recv"].at[m], "qkv_sem", m, y_dev)
 
         for m in range(3):
-            if not pre and m > 0:
+            if not pre:
                 flatten(m)
             for j in range(heads * hd // 256):
                 cols = slice(j * 256, (j + 1) * 256)
@@ -380,9 +397,13 @@
             reverse_rel()
         operand["bias_u"].wait()
         operand["bias_w"].wait()
+        sum_copy(2).wait()
+        for j, f in enumerate(factors(r["ss_send"][2], r["ss_recv"][2], batch)):
+            r["fac"][j] = jnp.broadcast_to(f, (batch, 128))
+        own_fac, peer_fac = (r["fac"][j, mine][:, 0:1] for j in range(2))
         for m in range(3):
             swap(m).wait()
-            full = (r["qkv_own"][m].astype(F32) + r["qkv_recv"][m].astype(F32)).astype(BF).astype(F32)
+            full = (r["qkv_own"][m].astype(F32) * own_fac + r["qkv_recv"][m].astype(F32) * peer_fac).astype(BF).astype(F32)
             for hh in range(heads):
                 head = full[:, hh * hd:(hh + 1) * hd]
                 if m:
@@ -407,7 +428,8 @@
     ins = [("hidden", hidden)]
     placed = {"ctx"} if layer == 0 else {"ctx", "hidden"}
     outs = []
-    scratch = [("ss_send", pltpu.VMEM((2, 8, 128), F32)), ("ss_recv", pltpu.VMEM((2, 3, 8, 128), F32)), ("ss_sem", dma((2, 2, 3))),
+    scratch = [("ss_send", pltpu.VMEM((3, 8, 128), F32)), ("ss_recv", pltpu.VMEM((3, 8, 128), F32)), ("ss_sem", dma((2, 3))),
+               ("fac", pltpu.VMEM((2, batch, 128), F32)),
                ("h", pltpu.VMEM((batch, width), BF)), ("part", pltpu.VMEM((batch, half), F32)),
                ("op_sem", dma((6,))),
                ("wup", pltpu.VMEM((width, ff if pre else 3 * flat), BF))]
@@ -420,11 +442,11 @@
         scratch += [("v_g_mlp", gain),
                     ("wo", pltpu.VMEM((flat, width), BF)), ("wo_sem", dma((4,))), ("wup_sem", dma((n_up,))),
                     ("wdn", pltpu.VMEM((ff, width), BF)), ("wdn_sem", dma((n_up,))),
-                    ("pair_send", part), ("pair_recv", part), ("pair_sem", dma((2, 2, PIECES))),
-                    ("chip_send", part), ("chip_recv", part), ("chip_sem", dma((2, 2, PIECES))), ("share_sem", dma((2, 2, PIECES))),
+                    ("pair_send", part), ("pair_recv", part), ("pair_sem", dma((2, 3, 4))),
+                    ("chip_send", part), ("chip_recv", part), ("chip_sem", dma((2, 3, 4))), ("share_sem", dma((2, 3, 4))),
                     ("ctx_all", pltpu.VMEM((batch, flat), BF)), ("ctx_sem", dma((2, 1))),
                     ("x_mid", pltpu.VMEM((batch, width), BF)), ("x_end", pltpu.VMEM((batch, width), BF)),
-                    ("up_send", pltpu.VMEM((batch, ff), BF)), ("up_recv", pltpu.VMEM((batch, ff), BF)), ("up_sem", dma((2, n_up))),
+                    ("up_send", pltpu.VMEM((batch, ff), BF)), ("up_recv", pltpu.VMEM((batch, ff), BF)), ("up_sem", dma((2, 2, n_up))),
                     ("act", pltpu.VMEM((batch, UP_CHUNK), BF)), ("acc", pltpu.VMEM((batch, width), F32))]
     if qkv:
         ins += [("g_attn", w["norm_attn"]), ("w_q", w["w_q"]), ("w_k", w["w_k"]), ("w_v", w["w_v"]), ("k_cache", w["k_cache"]), ("v_cache", w["v_cache"])]

time: 114 us -> 105 us (0.921)
  Pallas kernels: 112 us -> 104 us
    pallas_call x3, Pallas kernels: 98.2 us -> 89.9 us  [stage(): pl.pallas_call(functools.partial(stage_body, pre, qkv, layer, names), out...]
where the time goes in v5:
time: 105 us
  Pallas kernels  104 us (99%)
    pallas_call x3, Pallas kernels, stage(): pl.pallas_call(functools.partial(stage_body, pre, qkv, layer, names), out...  89.9 us
    pallas_call x2, Pallas kernels, attend_cache(): pl.pallas_call(functools.partial(attn_body, layer, group), out_shape=(plt...  13.9 us

profile of v5, /device:TPU:0, one launch (start us, length us, event | category | flops | bytes accessed | tf_op | source)
XLA Modules:
  0.0 105.2 jit_solution(3991589170869588051)
XLA Ops:
  0.6 0.0 copy-start
  0.6 16.1 %stage_01.1 = (f32[32,8,128]{2,1,0:T(8,128)S(1)}, f32[32,8,128]{2,1,0:T(8,128)S(1)}, f32[32,8,128]{2,1,0:T(8,128)S(1)}, f32[32,8,128]{2,1,0:T(8,128)S(1)}, bf16[...) custom-call(bf16[64,2048]{1,0:T(8,128)(2,1)} %refs_0_.3, ...), custom_call_target="tpu_custom_call" | custom-call | tf_op jit(solution)/shard_map/stage_01/pallas_call | solution.py:466
  16.7 0.0 copy-done
  16.8 6.9 %attend_0.1 = (f32[32,8,128]{2,1,0:T(8,128)S(1)}, bf16[2,32,1024,128]{3,2,1,0:T(8,128)(2,1)}, bf16[2,32,1024,128]{3,2,1,0:T(8,128)(2,1)}, bf16[32,1024,128]{2,1,0:T(8,128)(2,1)S(1)}, bf16[32,1024,128]{2,1,0:T(8,128)(2,1)S(1)}) custom-call(s32[64]{0:T(128)S(1)} %copy-done, ...), custom_call_target="tpu_custom_call", output_to_operand_aliasing={{3}: (6, {}), {4}: (7, {})} | custom-call | tf_op jit(solution)/shard_map/attend_0/pallas_call | solution.py:85
  23.7 42.3 %stage_11.1 = (bf16[64,2048]{1,0:T(8,128)(2,1)S(1)}, f32[32,8,128]{2,1,0:T(8,128)S(1)}, f32[32,8,128]{2,1,0:T(8,128)S(1)}, f32[32,8,128]{2,1,0:T(8,128)S(1)}, f3...) custom-call(bf16[64,2048]{1,0:T(8,128)(2,1)} %refs_0_.3, ...), custom_call_target="tpu_custom_call" | custom-call | tf_op jit(solution)/shard_map/stage_11/pallas_call | solution.py:466
  66.0 6.9 %attend_1.1 = (f32[32,8,128]{2,1,0:T(8,128)S(1)}, bf16[2,32,1024,128]{3,2,1,0:T(8,128)(2,1)}, bf16[2,32,1024,128]{3,2,1,0:T(8,128)(2,1)}, bf16[32,1024,128]{2,1,0:T(8,128)(2,1)S(1)}, bf16[32,1024,128]{2,1,0:T(8,128)(2,1)S(1)}) custom-call(s32[64]{0:T(128)S(1)} %copy-done, ...), custom_call_target="tpu_custom_call", output_to_operand_aliasing={{3}: (6, {}), {4}: (7, {}), {1}: (8, {}), {2}: (9, {})} | custom-call | tf_op jit(solution)/shard_map/attend_1/pallas_call | solution.py:85
  72.9 31.5 %stage_10.1 = bf16[64,2048]{1,0:T(8,128)(2,1)S(1)} custom-call(bf16[64,2048]{1,0:T(8,128)(2,1)S(1)} %get-tuple-element.32.refs_0_, f32[32,8,128]{2,1,0:T(8,128)S(1)} %get-tuple-element.42.refs_1_, bf16[2,2048]{1,0:T(2,128)(2,1)} %refs_2_.5, bf16[2,1024,2048]{2,1,0:T(8,128)(2,1)} %bitcast.10, bf16[2,2048,4096]{2,1,0:T(8,128)(2,1)} %refs_4_.5, ...), custom_call_target="tpu_custom_call" | custom-call | tf_op jit(solution)/shard_map/stage_10/pallas_call | solution.py:466
  104.5 0.7 copy.31
Async XLA Ops:
  0.6 16.1 %copy-start = (s32[64]{0:T(128)S(1)}, s32[64]{0:T(128)}, u32[]{:S(2)}) copy-start(s32[64]{0:T(128)} %len_ref.3) | copy-start | bytes 772

commit v6 on v5

--- a/solution.py
+++ b/solution.py
@@ -94,7 +94,7 @@
 MESH = pl.DeviceIdType.MESH
 EPS = 1e-6
 UP_CHUNK = 512
-VMEM_LIMIT = 45875200
+VMEM_LIMIT = 46399488
 
 
 def rows_to_cols(col):
@@ -178,9 +178,22 @@
                 if after[0] < 3:
                     raw_copy(*after, j).start()
 
-        if m < 2:
+        if m < 2 and not pre:
             for c in cache_copies(m):
                 c.start()
+
+    def project(m, at, dst):
+        lanes = dst.shape[1]
+        for j in range(lanes // 256):
+            cols = slice(j * 256, (j + 1) * 256)
+            dst[:, cols] = jnp.dot(r["h"][at], r["wup"][:, m * lanes + j * 256:m * lanes + (j + 1) * 256], preferred_element_type=F32).astype(dst.dtype)
+
+    def swap(m):
+        return remote(r["qkv_send"].at[m], r["qkv_recv"].at[m], "qkv_sem", m, y_dev)
+
+    def send_rows(m):
+        project(m, theirs, r["qkv_send"].at[m])
+        swap(m).start()
 
     def reverse_rel():
         operand["rel"].wait()
@@ -218,19 +231,20 @@
     def sum_copy(slot):
         return remote(r["ss_send"].at[slot], r["ss_recv"].at[slot], "ss_sem", slot, y_dev)
 
-    def inv_rms(sums, n):
-        return lax.rsqrt(cols_to_rows(sums, n) / (2 * width) + EPS)
-
-    def normalize(slot, x_ref, at, n, gain_ref, gain_layer):
+    def inv_rms(sums):
+        return lax.rsqrt(cols_to_rows(sums, rows) / (2 * width) + EPS)
+
+    def normalize(slot, x_ref, at, gain_ref, gain_layer, send=True):
         wide = x_ref[at].astype(F32)
         r["ss_send"][slot] = rows_to_cols(row_sums(wide))
-        sum_copy(slot).start()
+        if send:
+            sum_copy(slot).start()
         gain = gain_ref[pl.ds(gain_layer, 1)].astype(F32)
-        r["h"][at] = (x_ref[at].astype(F32) * inv_rms(r["ss_send"][slot], n) * gain).astype(BF)
-
-    def factors(own_sums, peer_sums, n):
-        whole = inv_rms(own_sums + peer_sums, n)
-        return whole / inv_rms(own_sums, n), whole / inv_rms(peer_sums, n)
+        r["h"][at] = (x_ref[at].astype(F32) * inv_rms(r["ss_send"][slot]) * gain).astype(BF)
+
+    def factors(own_sums, peer_sums):
+        whole = inv_rms(own_sums + peer_sums)
+        return whole / jnp.maximum(inv_rms(own_sums), 1e-30), whole / jnp.maximum(inv_rms(peer_sums), 1e-30)
 
     def half_of(side):
         return pl.ds(pl.multiple_of(side * half, half), half)
@@ -243,13 +257,13 @@
             if kind == "share":
                 src = dst = out_ref.at[at, pl.ds(pl.multiple_of(core * half + c * step, step), step)]
             else:
-                src, dst = r[kind + "_send"].at[bank, at, here], r[kind + "_recv"].at[bank, at, here]
+                src, dst = r[kind + "_send"].at[at, here], r[kind + "_recv"].at[bank, at, here]
             sems = r[kind + "_sem"]
             return pltpu.make_async_remote_copy(src, dst, sems.at[0, slot, c], sems.at[1, slot, c],
                                                 device_id=chip_dev if kind == "chip" else pair_dev, device_id_type=MESH)
 
         def begin():
-            r["pair_send"][bank, at] = part_of(half_of(1 - core)).astype(BF)
+            r["pair_send"][at] = part_of(half_of(1 - core)).astype(BF)
             copy("pair").start()
             r["part"][at] = part_of(half_of(core))
 
@@ -257,7 +271,7 @@
             copy("pair").wait()
             for c in range(pieces):
                 here = slice(c * step, (c + 1) * step)
-                r["chip_send"][bank, at, here] = (r["part"][at, here] + r["pair_recv"][bank, at, here].astype(F32)).astype(BF)
+                r["chip_send"][at, here] = (r["part"][at, here] + r["pair_recv"][bank, at, here].astype(F32)).astype(BF)
                 copy("chip", c).start()
 
         def land():
@@ -265,7 +279,7 @@
                 copy("chip", c).wait()
                 here = slice(c * step, (c + 1) * step)
                 cols = pl.ds(pl.multiple_of(core * half + c * step, step), step)
-                total = r["chip_send"][bank, at, here].astype(F32) + r["chip_recv"][bank, at, here].astype(F32)
+                total = r["chip_send"][at, here].astype(F32) + r["chip_recv"][bank, at, here].astype(F32)
                 out_ref[at, cols] = (x_ref[at, cols].astype(F32) + total).astype(BF)
                 copy("share", c).start()
 
@@ -305,102 +319,125 @@
             operand["hidden"].wait()
         operand["g_mlp"].wait()
 
+        ff = r["wup"].shape[1]
+
         def exchange_up(g, at, i):
-            cols = pl.ds(pl.multiple_of(i * UP_CHUNK, UP_CHUNK), UP_CHUNK)
+            cols = pl.ds(i * UP_CHUNK, UP_CHUNK)
             return pltpu.make_async_remote_copy(r["up_send"].at[at, cols], r["up_recv"].at[at, cols], r["up_sem"].at[0, g, i], r["up_sem"].at[1, g, i],
                                                 device_id=y_dev, device_id_type=MESH)
 
-        def send_up(g, at):
-            normalize(g, r["x_mid"], at, rows, r["v_g_mlp"], layer)
-
-            @pl.loop(0, n_up)
-            def _(i):
-                if g == 0:
+        def send_up(g, at, first, end):
+            cols = slice(first * UP_CHUNK, end * UP_CHUNK)
+            if g == 0:
+                for i in range(first, end):
                     up_copy(i).wait()
-                cols = pl.ds(pl.multiple_of(i * UP_CHUNK, UP_CHUNK), UP_CHUNK)
-                r["up_send"][at, cols] = jnp.dot(r["h"][at], r["wup"][:, cols], preferred_element_type=F32).astype(BF)
+            r["up_send"][at, cols] = jnp.dot(r["h"][at], r["wup"][:, cols], preferred_element_type=F32).astype(BF)
+            for i in range(first, end):
                 exchange_up(g, at, i).start()
 
         near[2]()
         near[3]()
-        send_up(0, mine)
+        normalize(0, r["x_mid"], mine, r["v_g_mlp"], layer)
+        quarter = n_up // 4
+        send_up(0, mine, 0, 1)
+        send_up(0, mine, 1, quarter)
+        send_up(0, mine, quarter, 2 * quarter)
         far[2]()
+        send_up(0, mine, 2 * quarter, 3 * quarter)
+        send_up(0, mine, 3 * quarter, n_up)
         far[3]()
-        send_up(1, theirs)
+        normalize(1, r["x_mid"], theirs, r["v_g_mlp"], layer)
+        send_up(1, theirs, 0, quarter)
+        send_up(1, theirs, quarter, 2 * quarter)
+        send_up(1, theirs, 2 * quarter, n_up)
 
         if qkv:
-            flatten(0)
+            for c in cache_copies(0) + cache_copies(1):
+                c.start()
 
         for g in range(2):
             sum_copy(g).wait()
         for g, at in enumerate((mine, theirs)):
-            for j, f in enumerate(factors(r["ss_send"][g], r["ss_recv"][1 - g], rows)):
+            for j, f in enumerate(factors(r["ss_send"][g], r["ss_recv"][1 - g])):
                 r["fac"][j, at] = jnp.broadcast_to(f, (rows, 128))
 
-        def activate(i):
-            cols = pl.ds(pl.multiple_of(i * UP_CHUNK, UP_CHUNK), UP_CHUNK)
-            exchange_up(0, mine, i).wait()
-            exchange_up(1, theirs, i).wait()
-            m = r["up_send"][:, cols].astype(F32) * r["fac"][0][:, 0:1] + r["up_recv"][:, cols].astype(F32) * r["fac"][1][:, 0:1]
-            r["act"][...] = jax.nn.gelu(m.astype(BF).astype(F32), approximate=True).astype(BF)
-
-        r["acc"][...] = jnp.zeros_like(r["acc"])
-
-        @pl.loop(0, n_up - 1)
-        def _(i):
-            down_copy(i).wait()
-            activate(i)
-            sl = pl.ds(pl.multiple_of(i * UP_CHUNK, UP_CHUNK), UP_CHUNK)
-            r["acc"][...] += jnp.dot(r["act"][...], r["wdn"][sl, :], preferred_element_type=F32)
-
-        down_copy(n_up - 1).wait()
-        activate(n_up - 1)
-
-        def down_part(cols):
-            last = jnp.dot(r["act"][...], r["wdn"][pl.ds((n_up - 1) * UP_CHUNK, UP_CHUNK), cols], preferred_element_type=F32)
-            return r["acc"][:, cols] + last
-
-        begin, cross, land, finish = reducer(2, 1, everyone, 4, down_part, r["x_mid"], r["x_end"])
-        begin()
-        cross()
+        def activate(g, at, first, end):
+            for i in range(first, end):
+                exchange_up(g, (mine, theirs)[g], i).wait()
+            cols = slice(first * UP_CHUNK, end * UP_CHUNK)
+            m = r["up_send"][at, cols].astype(F32) * r["fac"][0, at][:, 0:1] + r["up_recv"][at, cols].astype(F32) * r["fac"][1, at][:, 0:1]
+            r["up_recv"][at, cols] = jax.nn.gelu(m.astype(BF).astype(F32), approximate=True).astype(BF)
+
+        def consume(g, at, first, end):
+            if g == 0:
+                for i in range(first, end):
+                    down_copy(i).wait()
+            activate(g, at, first, end)
+            span = slice(first * UP_CHUNK, end * UP_CHUNK)
+            got = jnp.dot(r["up_recv"][at, span], r["wdn"][span, :], preferred_element_type=F32)
+            r["acc"][at] = got if first == 0 else r["acc"][at] + got
+
+        def last_part(cols):
+            span = slice(3 * quarter * UP_CHUNK, ff)
+            return r["acc"][mine, cols] + jnp.dot(r["up_recv"][mine, span], r["wdn"][span, cols], preferred_element_type=F32)
+
+        x_now = r["x_end"]
+        far = reducer(2, 1, theirs, 2, lambda cols: r["acc"][theirs, cols], r["x_mid"], r["x_end"])
+        near = reducer(3, 1, mine, 2, last_part, r["x_mid"], r["x_end"])
+        consume(0, theirs, 0, n_up)
+        far[0]()
+        consume(1, mine, 0, 2 * quarter)
+        far[1]()
+        consume(1, mine, 2 * quarter, 3 * quarter)
+        activate(1, mine, 3 * quarter, n_up)
+        near[0]()
+        if not qkv:
+            near[1]()
+            far[2]()
+            far[3]()
+        else:
+            near[1]()
+            far[2]()
+            flatten(0)
+            far[3]()
+            operand["g_attn"].wait()
+            normalize(2, x_now, theirs, r["v_g_attn"], qkv_layer)
+            send_rows(0)
+            flatten(1)
+            send_rows(1)
+        near[2]()
         if qkv:
-            flatten(1)
             flatten(2)
-            reverse_rel()
-        land()
-        finish()
+        near[3]()
         r["x_out"][...] = r["x_end"][...]
-        x_now = r["x_end"]
 
     if qkv:
         heads, hd = r["wraw"].shape[2:]
-        operand["g_attn"].wait()
         if not pre:
+            operand["g_attn"].wait()
             operand["hidden"].wait()
-        normalize(2, x_now, everyone, batch, r["v_g_attn"], qkv_layer)
-
-        def swap(m):
-            return remote(r["qkv_send"].at[m], r["qkv_recv"].at[m], "qkv_sem", m, y_dev)
-
-        for m in range(3):
-            if not pre:
+            normalize(2, x_now, theirs, r["v_g_attn"], qkv_layer)
+        normalize(3, x_now, mine, r["v_g_attn"], qkv_layer, send=False)
+        if pre:
+            project(2, everyone, r["part"])
+            r["qkv_send"][2] = r["part"][theirs].astype(BF)
+            swap(2).start()
+            r["qkv_own"][2] = r["part"][mine].astype(BF)
+        if not pre:
+            for m in range(3):
                 flatten(m)
-            for j in range(heads * hd // 256):
-                cols = slice(j * 256, (j + 1) * 256)
-                lanes = slice(m * heads * hd + j * 256, m * heads * hd + (j + 1) * 256)
-                r["part"][:, cols] = jnp.dot(r["h"][...], r["wup"][:, lanes], preferred_element_type=F32)
-            r["qkv_send"][m] = r["part"][theirs, :].astype(BF)
-            swap(m).start()
-            r["qkv_own"][m] = r["part"][mine, :].astype(BF)
-
-        if not pre:
-            reverse_rel()
+                project(m, everyone, r["part"])
+                r["qkv_send"][m] = r["part"][theirs].astype(BF)
+                swap(m).start()
+                r["qkv_own"][m] = r["part"][mine].astype(BF)
+        else:
+            for m in range(2):
+                project(m, mine, r["qkv_own"].at[m])
+        reverse_rel()
         operand["bias_u"].wait()
         operand["bias_w"].wait()
         sum_copy(2).wait()
-        for j, f in enumerate(factors(r["ss_send"][2], r["ss_recv"][2], batch)):
-            r["fac"][j] = jnp.broadcast_to(f, (batch, 128))
-        own_fac, peer_fac = (r["fac"][j, mine][:, 0:1] for j in range(2))
+        own_fac, peer_fac = factors(r["ss_send"][3], r["ss_recv"][2])
         for m in range(3):
             swap(m).wait()
             full = (r["qkv_own"][m].astype(F32) * own_fac + r["qkv_recv"][m].astype(F32) * peer_fac).astype(BF).astype(F32)
@@ -428,7 +465,7 @@
     ins = [("hidden", hidden)]
     placed = {"ctx"} if layer == 0 else {"ctx", "hidden"}
     outs = []
-    scratch = [("ss_send", pltpu.VMEM((3, 8, 128), F32)), ("ss_recv", pltpu.VMEM((3, 8, 128), F32)), ("ss_sem", dma((2, 3))),
+    scratch = [("ss_send", pltpu.VMEM((4, 8, 128), F32)), ("ss_recv", pltpu.VMEM((3, 8, 128), F32)), ("ss_sem", dma((2, 3))),
                ("fac", pltpu.VMEM((2, batch, 128), F32)),
                ("h", pltpu.VMEM((batch, width), BF)), ("part", pltpu.VMEM((batch, half), F32)),
                ("op_sem", dma((6,))),
@@ -442,12 +479,12 @@
         scratch += [("v_g_mlp", gain),
                     ("wo", pltpu.VMEM((flat, width), BF)), ("wo_sem", dma((4,))), ("wup_sem", dma((n_up,))),
                     ("wdn", pltpu.VMEM((ff, width), BF)), ("wdn_sem", dma((n_up,))),
-                    ("pair_send", part), ("pair_recv", part), ("pair_sem", dma((2, 3, 4))),
-                    ("chip_send", part), ("chip_recv", part), ("chip_sem", dma((2, 3, 4))), ("share_sem", dma((2, 3, 4))),
+                    ("pair_send", pltpu.VMEM((batch, half), BF)), ("pair_recv", part), ("pair_sem", dma((2, 4, 4))),
+                    ("chip_send", pltpu.VMEM((batch, half), BF)), ("chip_recv", part), ("chip_sem", dma((2, 4, 4))), ("share_sem", dma((2, 4, 4))),
                     ("ctx_all", pltpu.VMEM((batch, flat), BF)), ("ctx_sem", dma((2, 1))),
                     ("x_mid", pltpu.VMEM((batch, width), BF)), ("x_end", pltpu.VMEM((batch, width), BF)),
                     ("up_send", pltpu.VMEM((batch, ff), BF)), ("up_recv", pltpu.VMEM((batch, ff), BF)), ("up_sem", dma((2, 2, n_up))),
-                    ("act", pltpu.VMEM((batch, UP_CHUNK), BF)), ("acc", pltpu.VMEM((batch, width), F32))]
+                    ("acc", pltpu.VMEM((batch, width), F32))]
     if qkv:
         ins += [("g_attn", w["norm_attn"]), ("w_q", w["w_q"]), ("w_k", w["w_k"]), ("w_v", w["w_v"]), ("k_cache", w["k_cache"]), ("v_cache", w["v_cache"])]
         ins += [("rel", w["rel"]), ("bias_u", w["bias_u"]), ("bias_w", w["bias_w"])]

time: 105 us -> 101 us (0.962)
  Pallas kernels: 104 us -> 99.7 us
    pallas_call x3, Pallas kernels: 89.9 us -> 85.9 us  [stage(): pl.pallas_call(functools.partial(stage_body, pre, qkv, layer, names), out...]
where the time goes in v6:
time: 101 us
  Pallas kernels  99.7 us (99%)
    pallas_call x3, Pallas kernels, stage(): pl.pallas_call(functools.partial(stage_body, pre, qkv, layer, names), out...  85.9 us
    pallas_call x2, Pallas kernels, attend_cache(): pl.pallas_call(functools.partial(attn_body, layer, group), out_shape=(plt...  13.9 us

profile of v6, /device:TPU:0, one launch (start us, length us, event | category | flops | bytes accessed | tf_op | source)
XLA Modules:
  0.0 101.1 jit_solution(14558183981370848031)
XLA Ops:
  0.6 0.0 copy-start
  0.6 16.2 %stage_01.1 = (f32[32,8,128]{2,1,0:T(8,128)S(1)}, f32[32,8,128]{2,1,0:T(8,128)S(1)}, f32[32,8,128]{2,1,0:T(8,128)S(1)}, f32[32,8,128]{2,1,0:T(8,128)S(1)}, bf16[...) custom-call(bf16[64,2048]{1,0:T(8,128)(2,1)} %refs_0_.3, ...), custom_call_target="tpu_custom_call" | custom-call | tf_op jit(solution)/shard_map/stage_01/pallas_call | solution.py:503
  16.9 0.0 copy-done
  16.9 6.9 %attend_0.1 = (f32[32,8,128]{2,1,0:T(8,128)S(1)}, bf16[2,32,1024,128]{3,2,1,0:T(8,128)(2,1)}, bf16[2,32,1024,128]{3,2,1,0:T(8,128)(2,1)}, bf16[32,1024,128]{2,1,0:T(8,128)(2,1)S(1)}, bf16[32,1024,128]{2,1,0:T(8,128)(2,1)S(1)}) custom-call(s32[64]{0:T(128)S(1)} %copy-done, ...), custom_call_target="tpu_custom_call", output_to_operand_aliasing={{3}: (6, {}), {4}: (7, {})} | custom-call | tf_op jit(solution)/shard_map/attend_0/pallas_call | solution.py:85
  23.8 39.8 %stage_11.1 = (bf16[64,2048]{1,0:T(8,128)(2,1)S(1)}, f32[32,8,128]{2,1,0:T(8,128)S(1)}, f32[32,8,128]{2,1,0:T(8,128)S(1)}, f32[32,8,128]{2,1,0:T(8,128)S(1)}, f3...) custom-call(bf16[64,2048]{1,0:T(8,128)(2,1)} %refs_0_.3, ...), custom_call_target="tpu_custom_call" | custom-call | tf_op jit(solution)/shard_map/stage_11/pallas_call | solution.py:503
  63.6 6.9 %attend_1.1 = (f32[32,8,128]{2,1,0:T(8,128)S(1)}, bf16[2,32,1024,128]{3,2,1,0:T(8,128)(2,1)}, bf16[2,32,1024,128]{3,2,1,0:T(8,128)(2,1)}, bf16[32,1024,128]{2,1,0:T(8,128)(2,1)S(1)}, bf16[32,1024,128]{2,1,0:T(8,128)(2,1)S(1)}) custom-call(s32[64]{0:T(128)S(1)} %copy-done, ...), custom_call_target="tpu_custom_call", output_to_operand_aliasing={{3}: (6, {}), {4}: (7, {}), {1}: (8, {}), {2}: (9, {})} | custom-call | tf_op jit(solution)/shard_map/attend_1/pallas_call | solution.py:85
  70.6 29.8 %stage_10.1 = bf16[64,2048]{1,0:T(8,128)(2,1)S(1)} custom-call(bf16[64,2048]{1,0:T(8,128)(2,1)S(1)} %get-tuple-element.32.refs_0_, f32[32,8,128]{2,1,0:T(8,128)S(1)} %get-tuple-element.42.refs_1_, bf16[2,2048]{1,0:T(2,128)(2,1)} %refs_2_.5, bf16[2,1024,2048]{2,1,0:T(8,128)(2,1)} %bitcast.10, bf16[2,2048,4096]{2,1,0:T(8,128)(2,1)} %refs_4_.5, ...), custom_call_target="tpu_custom_call" | custom-call | tf_op jit(solution)/shard_map/stage_10/pallas_call | solution.py:503
  100.4 0.7 copy.31
Async XLA Ops:
  0.6 16.3 %copy-start = (s32[64]{0:T(128)S(1)}, s32[64]{0:T(128)}, u32[]{:S(2)}) copy-start(s32[64]{0:T(128)} %len_ref.3) | copy-start | bytes 772

commit v7 on v6

--- a/solution.py
+++ b/solution.py
@@ -67,7 +67,7 @@
             c.wait()
 
 
-def attend_cache(layer, lengths, fed, layers, prev, group=8):
+def attend_cache(layer, lengths, fed, layers, prev, group=16):
     rows, span, hd = fed[-1].shape
     heads = fed[0].shape[1]
     any_ = pl.BlockSpec(memory_space=pltpu.HBM)

time: 101 us -> 101 us (level)
  no operation moved by 1% of the time
where the time goes in v7:
time: 101 us; the launch traced here: 100 us
  Pallas kernels  99.1 us (98%)
    pallas_call x3, Pallas kernels, stage(): pl.pallas_call(functools.partial(stage_body, pre, qkv, layer, names), out...  85.9 us
    pallas_call x2, Pallas kernels, attend_cache(): pl.pallas_call(functools.partial(attn_body, layer, group), out_shape=(plt...  13.2 us

profile of v7, /device:TPU:0, one launch (start us, length us, event | category | flops | bytes accessed | tf_op | source)
XLA Modules:
  0.0 100.5 jit_solution(7203251466557806523)
XLA Ops:
  0.6 0.0 copy-start
  0.6 16.2 %stage_01.1 = (f32[32,8,128]{2,1,0:T(8,128)S(1)}, f32[32,8,128]{2,1,0:T(8,128)S(1)}, f32[32,8,128]{2,1,0:T(8,128)S(1)}, f32[32,8,128]{2,1,0:T(8,128)S(1)}, bf16[...) custom-call(bf16[64,2048]{1,0:T(8,128)(2,1)} %refs_0_.3, ...), custom_call_target="tpu_custom_call" | custom-call | tf_op jit(solution)/shard_map/stage_01/pallas_call | solution.py:503
  16.9 0.0 copy-done
  16.9 6.6 %attend_0.1 = (f32[32,8,128]{2,1,0:T(8,128)S(1)}, bf16[2,32,1024,128]{3,2,1,0:T(8,128)(2,1)}, bf16[2,32,1024,128]{3,2,1,0:T(8,128)(2,1)}, bf16[32,1024,128]{2,1,0:T(8,128)(2,1)S(1)}, bf16[32,1024,128]{2,1,0:T(8,128)(2,1)S(1)}) custom-call(s32[64]{0:T(128)S(1)} %copy-done, ...), custom_call_target="tpu_custom_call", output_to_operand_aliasing={{3}: (6, {}), {4}: (7, {})} | custom-call | tf_op jit(solution)/shard_map/attend_0/pallas_call | solution.py:85
  23.5 39.8 %stage_11.1 = (bf16[64,2048]{1,0:T(8,128)(2,1)S(1)}, f32[32,8,128]{2,1,0:T(8,128)S(1)}, f32[32,8,128]{2,1,0:T(8,128)S(1)}, f32[32,8,128]{2,1,0:T(8,128)S(1)}, f3...) custom-call(bf16[64,2048]{1,0:T(8,128)(2,1)} %refs_0_.3, ...), custom_call_target="tpu_custom_call" | custom-call | tf_op jit(solution)/shard_map/stage_11/pallas_call | solution.py:503
  63.3 6.6 %attend_1.1 = (f32[32,8,128]{2,1,0:T(8,128)S(1)}, bf16[2,32,1024,128]{3,2,1,0:T(8,128)(2,1)}, bf16[2,32,1024,128]{3,2,1,0:T(8,128)(2,1)}, bf16[32,1024,128]{2,1,0:T(8,128)(2,1)S(1)}, bf16[32,1024,128]{2,1,0:T(8,128)(2,1)S(1)}) custom-call(s32[64]{0:T(128)S(1)} %copy-done, ...), custom_call_target="tpu_custom_call", output_to_operand_aliasing={{3}: (6, {}), {4}: (7, {}), {1}: (8, {}), {2}: (9, {})} | custom-call | tf_op jit(solution)/shard_map/attend_1/pallas_call | solution.py:85
  70.0 29.8 %stage_10.1 = bf16[64,2048]{1,0:T(8,128)(2,1)S(1)} custom-call(bf16[64,2048]{1,0:T(8,128)(2,1)S(1)} %get-tuple-element.32.refs_0_, f32[32,8,128]{2,1,0:T(8,128)S(1)} %get-tuple-element.42.refs_1_, bf16[2,2048]{1,0:T(2,128)(2,1)} %refs_2_.5, bf16[2,1024,2048]{2,1,0:T(8,128)(2,1)} %bitcast.10, bf16[2,2048,4096]{2,1,0:T(8,128)(2,1)} %refs_4_.5, ...), custom_call_target="tpu_custom_call" | custom-call | tf_op jit(solution)/shard_map/stage_10/pallas_call | solution.py:503
  99.8 0.7 copy.31
Async XLA Ops:
  0.6 16.3 %copy-start = (s32[64]{0:T(128)S(1)}, s32[64]{0:T(128)}, u32[]{:S(2)}) copy-start(s32[64]{0:T(128)} %len_ref.3) | copy-start | bytes 772
